TPU v7x, 128 devices: a whole 4x4x4 slice. The times are simulated.
128 devices in a mesh: replica: 16 (over z, y), data: 8 (over x, core).
Axes of the slice: x: 4, y: 4, z: 4, core: 2. Of those that a mesh axis runs over, the one named last changes fastest.
Arguments:
- img_x: bfloat16 [32768, 2048], P(('replica', 'data'))
- txt_x: bfloat16 [32768, 512], P(('replica', 'data'))
- w_img: bfloat16 [2048, 1024], replicated
- w_txt: bfloat16 [512, 1024], replicated
- log_temp: float32 [1], replicated
- logit_bias: float32 [1], replicated
Outputs:
- output 1: float32 [1], replicated
- output 2: float32 [1], replicated
- output 3: float32 [1], replicated
- output 4: float32 [2048, 1024], replicated
- output 5: float32 [512, 1024], replicated
All inputs are finite; a program needn't handle non-finite values.
Results may differ from a plain program's by a relative error of at most 0.001.
Values are sent between devices in bfloat16 or wider.
A program may use at most 1 GiB of HBM per device.

v0:
```python
import jax
import jax.numpy as jnp
from jax import lax
from jax.sharding import PartitionSpec as P


def normalize(raw):
    return raw * lax.rsqrt(jnp.sum(raw * raw, axis=-1, keepdims=True))


def embed_rows(feat_x, w_proj):
    raw_emb = jnp.dot(feat_x, w_proj, preferred_element_type=jnp.float32)
    unit_emb, pull_back = jax.vjp(normalize, raw_emb)
    return unit_emb.astype(jnp.bfloat16), pull_back


def tile_terms(img_emb, txt_blk, labels, temp_scale, bias_val, total_rows):
    sim_tile = jnp.einsum("id,jd->ij", img_emb, txt_blk, preferred_element_type=jnp.float32)
    logits = temp_scale * sim_tile + bias_val
    loss_part = -jnp.sum(jax.nn.log_sigmoid(labels * logits))
    grad_tile = -labels * jax.nn.sigmoid(-labels * logits) / total_rows
    grad_b = grad_tile.astype(jnp.bfloat16)
    d_img = jnp.dot(grad_b, txt_blk, preferred_element_type=jnp.float32)
    d_txt = jnp.einsum("ij,id->jd", grad_b, img_emb, preferred_element_type=jnp.float32)
    return loss_part, jnp.sum(grad_tile * sim_tile), jnp.sum(grad_tile), d_img, d_txt


def solution(mesh):
    rep_count = mesh.shape["replica"]
    data_count = mesh.shape["data"]
    dev_count = rep_count * data_count
    batch_axes = ("replica", "data")
    next_perm = [(k, (k + 1) % dev_count) for k in range(dev_count)]

    def local_fn(img_x, txt_x, w_img, w_txt, log_temp, logit_bias):
        local_rows = img_x.shape[0]
        total_rows = local_rows * dev_count
        img_emb, img_pull = embed_rows(img_x, w_img)
        txt_emb, txt_pull = embed_rows(txt_x, w_txt)
        temp_scale = jnp.exp(log_temp[0])
        bias_val = logit_bias[0]
        row_ids = lax.broadcasted_iota(jnp.int32, (local_rows, 1), 0)
        col_ids = lax.broadcasted_iota(jnp.int32, (1, local_rows), 1)
        diag_labels = jnp.where(row_ids == col_ids, 1.0, -1.0)
        first = tile_terms(img_emb, txt_emb, diag_labels, temp_scale, bias_val, total_rows)

        def hop(step, state):
            txt_blk, d_txt_acc, d_img_acc, loss_acc, temp_acc, bias_acc = state
            txt_blk = lax.ppermute(txt_blk, batch_axes, next_perm)
            d_txt_acc = lax.ppermute(d_txt_acc, batch_axes, next_perm)
            loss_part, temp_part, bias_part, d_img_part, d_txt_part = tile_terms(img_emb, txt_blk, -1.0, temp_scale, bias_val, total_rows)
            return (txt_blk, d_txt_acc + d_txt_part, d_img_acc + d_img_part, loss_acc + loss_part, temp_acc + temp_part, bias_acc + bias_part)

        init_state = (txt_emb, first[4], first[3], first[0], first[1], first[2])
        final_state = lax.fori_loop(1, dev_count, hop, init_state)
        d_txt_home = lax.ppermute(final_state[1], batch_axes, next_perm)
        d_img_raw = img_pull(temp_scale * final_state[2])[0].astype(jnp.bfloat16)
        d_txt_raw = txt_pull(temp_scale * d_txt_home)[0].astype(jnp.bfloat16)
        d_w_img = jnp.einsum("nf,nd->fd", img_x, d_img_raw, preferred_element_type=jnp.float32)
        d_w_txt = jnp.einsum("nf,nd->fd", txt_x, d_txt_raw, preferred_element_type=jnp.float32)
        loss_total, temp_total, bias_total, d_w_img, d_w_txt = lax.psum((final_state[3], final_state[4], final_state[5], d_w_img, d_w_txt), batch_axes)
        loss_out = jnp.reshape(loss_total / total_rows, (1,))
        d_log_temp = jnp.reshape(temp_scale * temp_total, (1,))
        d_logit_bias = jnp.reshape(bias_total, (1,))
        return loss_out, d_log_temp, d_logit_bias, d_w_img, d_w_txt

    batch_spec = P(batch_axes, None)
    return jax.shard_map(local_fn, mesh=mesh, in_specs=(batch_spec, batch_spec, P(), P(), P(), P()), out_specs=(P(), P(), P(), P(), P()), check_vma=False)
```

profile of v0, /device:TPU:1, one launch (start us, length us, event | category | flops | bytes accessed | tf_op | source)
XLA Modules:
  0.0 4032.9 jit_solution(13850366801978953599)
XLA Ops:
  16.0 3800.7 %while.20 = (s32[]{:T(128)}, bf16[256,1024]{1,0:T(8,128)(2,1)}, f32[256,1024]{1,0:T(8,128)}, f32[256,1024]{1,0:T(8,128)S(1)}, f32[]{:T(128)}, /*index=5*/f32[]{:...) while((s32[]{:T(128)}, bf16[256,1024]{1,0:T(8,128)(2,1)}, ...), condition=%wide.region_9.10_spmd, body=%wide.region_5.9_spmd.sunk | while | flops 405274624 | bytes 14418181 | solution.py:55
  302.2 18.0 collective-permute-done
  422.3 18.0 collective-permute-done
  542.5 18.0 collective-permute-done
  662.6 18.0 collective-permute-done
  782.8 18.0 collective-permute-done
  902.9 18.0 collective-permute-done
  1023.1 18.0 collective-permute-done
  1143.2 18.0 collective-permute-done
  1443.6 18.0 collective-permute-done
  1563.8 18.0 collective-permute-done
  1683.9 18.0 collective-permute-done
  1804.1 18.0 collective-permute-done
  1924.2 18.0 collective-permute-done
  2044.4 18.0 collective-permute-done
  2164.5 18.0 collective-permute-done
  2284.7 18.0 collective-permute-done
  2585.1 18.0 collective-permute-done
  2705.2 18.0 collective-permute-done
  2825.4 18.0 collective-permute-done
  2945.5 18.0 collective-permute-done
  3065.7 18.0 collective-permute-done
  3837.6 79.9 %all-reduce = (f32[]{:T(128)}, f32[]{:T(128)}, f32[1]{0:T(128)}) all-reduce(f32[]{:T(128)} %get-tuple-element.61, f32[]{:T(128)} %get-tuple-element.62, f32[1]{0:T(128)} %bitcast.4), channel_id=1, replica_groups=mesh['replica'=16,'data'=8] {'replica','data'}, use_global_device_ids=true, to_apply=%region_10.11 | all-reduce | flops 3 | bytes 24 | tf_op jit(solution)/shard_map/psum | solution.py:61
  3918.8 93.8 %all-reduce.4.cloned.1.call-done = (f32[2048,1024]{0,1:T(8,128)}, f32[512,1024]{0,1:T(8,128)}) async-done(((f32[2048,1024]{0,1:T(8,128)}, f32[512,1024]{0,1:T(8,128)}), (f32[2048,1024]{0,1:T(8,128)}, f32[512,1024]{0,1:T(8,128)})) %all-reduce.4.cloned.1.call-update) | async-done | bytes 10485776 | tf_op jit(solution)/shard_map/psum | solution.py:61
  (1033 shorter events, 2790.4 us)
Async XLA Ops:
  7.2 4005.4 %all-reduce.4.cloned.1.call-start = ((), (), s32[]{:S(2)}) async-start(), calls=%async_computation | async-start | bytes 20971520 | tf_op jit(solution)/shard_map/psum | solution.py:61
  122.0 25.3 collective-permute-start.1
  242.1 25.3 collective-permute-start.1
  362.3 25.3 collective-permute-start.1
  482.4 25.3 collective-permute-start.1
  542.5 25.3 collective-permute-start.1
  602.6 25.3 collective-permute-start.1
  662.6 25.3 collective-permute-start.1
  722.7 25.3 collective-permute-start.1
  782.8 25.3 collective-permute-start.1
  902.9 25.3 collective-permute-start.1
  1023.1 25.3 collective-permute-start.1
  1143.2 25.3 collective-permute-start.1
  1263.4 25.3 collective-permute-start.1
  1383.5 25.3 collective-permute-start.1
  1503.7 25.3 collective-permute-start.1
  1623.9 25.3 collective-permute-start.1
  1683.9 25.3 collective-permute-start.1
  1744.0 25.3 collective-permute-start.1
  1804.1 25.3 collective-permute-start.1
  1864.2 25.3 collective-permute-start.1
  1924.2 25.3 collective-permute-start.1
  2044.4 25.3 collective-permute-start.1
  2164.5 25.3 collective-permute-start.1
  (241 other events, 4952.1 us)
Sparse Core Ops, SparseCore 0:
  3837.7 174.8 all-reduce.3
where the time goes:
time: 4050 us; the launch traced here: 4030 us
  waiting for transfers between devices  2370 us (59%)
  matrix products  770 us (19%)
  loops' own time  671 us (17%)
  local copies, waits for them, and re-layouts  112 us (3%)
  blocking collectives  79.9 us (2%)
    ppermute x127, waiting for transfers between devices, hop(): txt_blk = lax.ppermute(txt_blk, batch_axes, next_perm)  2260 us
    another operation x1, loops' own time, local_fn(): final_state = lax.fori_loop(1, dev_count, hop, init_state)  671 us
    dot_general x128, matrix products, tile_terms(): jnp.einsum('ij,id->jd', grad_b, img_emb, preferred_element_type=jnp.float32)  408 us
    dot_general x128, matrix products, tile_terms(): jnp.einsum('id,jd->ij', img_emb, txt_blk, preferred_element_type=jnp.floa...  225 us
    dot_general x128, matrix products, tile_terms(): d_img = jnp.dot(grad_b, txt_blk, preferred_element_type=jnp.float32)  124 us
    while x127, local copies, waits for them, and re-layouts  101 us
    psum x1, waiting for transfers between devices, local_fn(): lax.psum((final_state[3], final_state[4], final_state[5], d_w_img, d_w_tx...  93.8 us
  transfers between devices with their start and end apart: 256, of which 131 were waited for; matrix products, arithmetic and copies ran while one was open for 11% of the time, Pallas kernels for 0%

commit v1 on v0

v1 whole, which is shorter than its diff:
```python
import functools

import jax
import jax.numpy as jnp
from jax import lax
from jax.experimental import pallas as pl
from jax.experimental.pallas import tpu as pltpu
from jax.sharding import PartitionSpec as P

TILE = 512
F32 = jnp.float32
BF16 = jnp.bfloat16


def normalize(raw):
    return raw * lax.rsqrt(jnp.sum(raw * raw, axis=-1, keepdims=True))


def embed_rows(feat_x, w_proj):
    raw_emb = jnp.dot(feat_x, w_proj, preferred_element_type=F32)
    unit_emb, pull_back = jax.vjp(normalize, raw_emb)
    return unit_emb.astype(BF16), pull_back


def score_terms(sim, scale, bias, diag):
    z = scale * sim + bias
    if diag is not None:
        z = jnp.where(diag, -z, z)
    e = jnp.exp(-jnp.abs(z))
    r = 1.0 / (1.0 + e)
    g = jnp.where(z >= 0.0, r, e * r)
    loss = jnp.maximum(z, 0.0) + jnp.log1p(e)
    if diag is not None:
        g = jnp.where(diag, -g, g)
    return loss, g


def fold(x):
    return jnp.sum(x.reshape(x.shape[0] // 8, 8, x.shape[1]), axis=0)


def tile_kernel(block, scal, img, img_t, txt, d_img, d_txt, sums):
    j = pl.program_id(0)
    rows = img.shape[0]
    scale, bias = scal[0], scal[1]
    rep, dat = lax.axis_index("replica"), lax.axis_index("data")

    @pl.when(j == 0)
    def _():
        d_img[...] = jnp.zeros_like(d_img)
        sums[...] = jnp.zeros_like(sums)

    def tile(i, masked):
        at = pl.ds(pl.multiple_of(i * TILE, TILE), TILE)
        sim = lax.dot_general(img[at, :], txt[...], (((1,), (1,)), ((), ())), preferred_element_type=F32)
        diag = None
        if masked:
            row = lax.broadcasted_iota(jnp.int32, sim.shape, 0) + (i * TILE - dat * block)
            col = lax.broadcasted_iota(jnp.int32, sim.shape, 1) + (j * TILE - rep * block)
            diag = (row == col) & (row >= 0) & (row < block)
        loss, g = score_terms(sim, scale, bias, diag)
        sums[0] += fold(loss)
        sums[1] += fold(g * sim)
        sums[2] += fold(g)
        gb = g.astype(BF16)
        d_img[at, :] += jnp.dot(gb, txt[...], preferred_element_type=F32)
        part = jnp.dot(img_t[:, at], gb, preferred_element_type=F32)

        @pl.when(i == 0)
        def _():
            d_txt[...] = part

        @pl.when(i > 0)
        def _():
            d_txt[...] += part

    per = TILE // block
    own_j = lax.div(rep, per) == j

    def step(i, carry):
        hit = own_j & (lax.div(dat, per) == i)

        @pl.when(hit)
        def _():
            tile(i, True)

        @pl.when(jnp.logical_not(hit))
        def _():
            tile(i, False)

        return carry

    lax.fori_loop(0, rows // TILE, step, 0)


def tile_call(block, scal, img, img_t, txt):
    rows, dim = img.shape
    cols = txt.shape[0]
    whole = pl.BlockSpec(memory_space=pltpu.VMEM)
    return pl.pallas_call(
        functools.partial(tile_kernel, block),
        grid=(cols // TILE,),
        in_specs=[pl.BlockSpec(memory_space=pltpu.SMEM), whole, whole, pl.BlockSpec((TILE, dim), lambda j: (j, 0))],
        out_specs=[whole, pl.BlockSpec((dim, TILE), lambda j: (0, j)), whole],
        out_shape=[
            jax.ShapeDtypeStruct((rows, dim), F32),
            jax.ShapeDtypeStruct((dim, cols), F32),
            jax.ShapeDtypeStruct((3, 8, TILE), F32),
        ],
        compiler_params=pltpu.CompilerParams(vmem_limit_bytes=60 * 2**20),
        cost_estimate=pl.CostEstimate(flops=6 * rows * cols * dim, bytes_accessed=4 * rows * dim + 8 * cols * dim, transcendentals=3 * rows * cols),
        name="tile",
    )(scal, img, img_t, txt)


def solution(mesh):
    rep_count = mesh.shape["replica"]
    data_count = mesh.shape["data"]
    batch_axes = ("replica", "data")

    def local_fn(img_x, txt_x, w_img, w_txt, log_temp, logit_bias):
        block = img_x.shape[0]
        dim = w_img.shape[1]
        total_rows = block * rep_count * data_count
        txt_emb, txt_pull = embed_rows(txt_x, w_txt)
        txt_all = lax.all_gather(txt_emb, "replica", axis=0, tiled=True)
        img_emb, img_pull = embed_rows(img_x, w_img)
        img_all = lax.all_gather(img_emb, "data", axis=0, tiled=True)
        temp_scale = jnp.exp(log_temp[0])
        scal = jnp.stack([temp_scale, logit_bias[0]])
        d_img, d_txt, sums = tile_call(block, scal, img_all, img_all.T, txt_all)
        d_txt = d_txt.reshape(dim, rep_count, block).transpose(1, 0, 2)
        d_txt = lax.psum_scatter(d_txt, "replica", scatter_dimension=0, tiled=False).T
        d_img = lax.psum_scatter(d_img, "data", scatter_dimension=0, tiled=True)
        post = temp_scale / total_rows
        d_img_raw = img_pull(post * d_img)[0].astype(BF16)
        d_txt_raw = txt_pull(post * d_txt)[0].astype(BF16)
        d_w_img = jnp.einsum("nf,nd->fd", img_x, d_img_raw, preferred_element_type=F32)
        d_w_txt = jnp.einsum("nf,nd->fd", txt_x, d_txt_raw, preferred_element_type=F32)
        parts = jnp.sum(sums, axis=(1, 2))
        parts, d_w_img, d_w_txt = lax.psum((parts, d_w_img, d_w_txt), batch_axes)
        parts = parts / total_rows
        return parts[0:1], temp_scale * parts[1:2], parts[2:3], d_w_img, d_w_txt

    batch_spec = P(batch_axes, None)
    return jax.shard_map(local_fn, mesh=mesh, in_specs=(batch_spec, batch_spec, P(), P(), P(), P()), out_specs=(P(), P(), P(), P(), P()), check_vma=False)
```

time: 4050 us -> 588 us (0.15)
  waiting for transfers between devices: 2370 us -> 340 us
  matrix products: 770 us -> 14.3 us
  loops' own time: 671 us -> 0 us
  Pallas kernels: 0 us -> 97.5 us
  local copies, waits for them, and re-layouts: 112 us -> 47.1 us
    ppermute x255 -> x0, waiting for transfers between devices: 2280 us -> none  [the longest x127 2260 us: hop(): txt_blk = lax.ppermute(txt_blk, batch_axes, next_perm)]
    dot_general x388 -> x4, matrix products: 770 us -> 14.3 us  [the longest x1 5.9 us: local_fn(): jnp.einsum('nf,nd->fd', img_x, d_img_raw, preferred_element_type=F32)]
    another operation x1 -> x0, loops' own time: 671 us -> none  [local_fn(): final_state = lax.fori_loop(1, dev_count, hop, init_state)]
    unnamed x1 -> x6, waiting for transfers between devices: 0.02 us -> 106 us
    all_gather x0 -> x2, waiting for transfers between devices: none -> 101 us  [the longest x1 67.4 us: local_fn(): txt_all = lax.all_gather(txt_emb, 'replica', axis=0, tiled=True)]
    while x127 -> x0, local copies, waits for them, and re-layouts: 101 us -> none
    pallas_call x0 -> x1, Pallas kernels: none -> 97.5 us  [tile_call(): pl.pallas_call(functools.partial(tile_kernel, block), grid=(cols // TILE,...]
  transfers between devices with their start and end apart: 256 -> 5, of which waited for: 131 -> 5; matrix products, arithmetic and copies ran while one was open for 11% -> 6% of each run, Pallas kernels for 0% -> 0%
where the time goes in v1:
time: 588 us; the launch traced here: 587 us
  waiting for transfers between devices  340 us (58%)
  Pallas kernels  97.5 us (17%)
  blocking collectives  65.7 us (11%)
  local copies, waits for them, and re-layouts  47.1 us (8%)
  between operations  17 us (3%)
  matrix products  14.3 us (2%)
    unnamed x6, waiting for transfers between devices  106 us
    psum x1, waiting for transfers between devices, local_fn(): parts, d_w_img, d_w_txt = lax.psum((parts, d_w_img, d_w_txt), batch_axes)  98.5 us
    pallas_call x1, Pallas kernels, tile_call(): pl.pallas_call(functools.partial(tile_kernel, block), grid=(cols // TILE,...  97.5 us
    all_gather x1, waiting for transfers between devices, local_fn(): txt_all = lax.all_gather(txt_emb, 'replica', axis=0, tiled=True)  67.4 us
    psum x1, blocking collectives, local_fn(): parts, d_w_img, d_w_txt = lax.psum((parts, d_w_img, d_w_txt), batch_axes)  65.7 us
    reduce_scatter x1, waiting for transfers between devices, local_fn(): d_img = lax.psum_scatter(d_img, 'data', scatter_dimension=0, tiled=True)  34.4 us
    all_gather x1, waiting for transfers between devices, local_fn(): img_all = lax.all_gather(img_emb, 'data', axis=0, tiled=True)  33.9 us
    reshape x1, local copies, waits for them, and re-layouts, local_fn(): d_txt = d_txt.reshape(dim, rep_count, block).transpose(1, 0, 2)  17.5 us
  transfers between devices with their start and end apart: 5, of which 5 were waited for; matrix products, arithmetic and copies ran while one was open for 6% of the time, Pallas kernels for 0%

profile of v1, /device:TPU:1, one launch (start us, length us, event | category | flops | bytes accessed | tf_op | source)
XLA Modules:
  0.0 587.4 jit_solution(11972764440626761575)
XLA Ops:
  7.2 1.2 copy-done
  8.4 3.5 multiply_reduce_fusion.2
  12.3 0.9 multiply_convert_fusion.1
  13.2 1.7 multiply_reduce_fusion.1
  15.0 0.9 multiply_convert_fusion
  17.3 0.6 pad_maximum_fusion.scal
  17.9 33.9 %all-gather.3.cloned.1.call-done = bf16[2048,1024]{0,1:T(8,128)(2,1)} async-done(((bf16[256,1024]{0,1:T(8,128)(2,1)}), bf16[2048,1024]{0,1:T(8,128)(2,1)}) %all-gather.3.cloned.1.call-update) | async-done | bytes 4194320 | tf_op jit(solution)/shard_map/all_gather | solution.py:128
  51.8 6.4 %copy.20.img = bf16[2048,1024]{1,0:T(8,128)(2,1)} copy(bf16[2048,1024]{0,1:T(8,128)(2,1)} %all-gather.3.cloned.1.call-done) | data formatting | bytes 8388608 | tf_op jit(solution)/shard_map/all_gather | solution.py:128
  58.2 67.4 %all-gather.5.cloned.1.call-done.txt = bf16[4096,1024]{1,0:T(8,128)(2,1)} async-done(((bf16[256,1024]{1,0:T(8,128)(2,1)}), bf16[4096,1024]{1,0:T(8,128)(2,1)}) %all-gather.5.cloned.1.call-update) | async-done | bytes 8388624 | tf_op jit(solution)/shard_map/all_gather | solution.py:126
  125.5 97.5 %tile.1 = (f32[2048,1024]{1,0:T(8,128)}, f32[1024,4096]{1,0:T(8,128)}, f32[3,8,512]{2,1,0:T(8,128)}) custom-call(f32[2]{0:T(128)} %pad_maximum_fusion.scal, bf16[2048,1024]{1,0:T(8,128)(2,1)} %copy.20.img, bf16[1024,2048]{1,0:T(8,128)(2,1)} %bitcast.27, bf16[4096,1024]{1,0:T(8,128)(2,1)} %all-gather.5.cloned.1.call-done.txt), custom_call_target="tpu_custom_call" | custom-call | flops 51539607552 | bytes 41943040 | tf_op jit(solution)/shard_map/tile/pallas_call | solution.py:100
  223.0 9.1 %copy.21 = f32[2048,1024]{0,1:T(8,128)} copy(f32[2048,1024]{1,0:T(8,128)} %get-tuple-element.9) | data formatting | bytes 16777216 | tf_op jit(solution)/shard_map/tile/pallas_call | solution.py:100
  232.2 17.5 %copy.27 = f32[1024,4096]{0,1:T(8,128)} copy(f32[1024,4096]{1,0:T(8,128)} %get-tuple-element.10) | data formatting | bytes 33554432 | tf_op jit(solution)/shard_map/reshape | solution.py:132
  249.8 34.4 %reduce-scatter.5.cloned.1.call-done = f32[256,1024]{0,1:T(8,128)} async-done(((f32[2048,1024]{0,1:T(8,128)}), f32[256,1024]{0,1:T(8,128)}) %reduce-scatter.5.cloned.1.call-update) | async-done | bytes 1048592 | tf_op jit(solution)/shard_map/reduce_scatter | solution.py:134
  284.2 1.4 multiply_reduce_fusion
  285.6 5.9 %convolution_bitcast_fusion = f32[2048,1024]{0,1:T(8,128)} fusion(bf16[256,2048]{1,0:T(8,128)(2,1)S(1)} %copy-done, f32[256,1024]{0,1:T(8,128)S(1)} %copy.19, f32[256,1024]{0,1:T(8,128)} %reduce-scatter.5.cloned.1.call-done, f32[256]{0:T(256)S(1)} %multiply_multiply_fusion.1, f32[]{:T(128)} %bitcast.1, f32[256]{0:T(256)S(1)} %rsqrt.20), kind=kOutput, calls=%fused_computation | convolution fusion | flops 1075314688 | bytes 11536388 | tf_op jit(solution)/shard_map/nf,nd->fd/dot_general | solution.py:138
  291.5 106.1 %reduce-scatter.7.cloned.1.call-done = f32[1,1024,256]{1,2,0:T(8,128)} async-done(((f32[16,1024,256]{1,2,0:T(8,128)}), f32[1,1024,256]{1,2,0:T(8,128)}) %reduce-scatter.7.cloned.1.call-update) | async-done | bytes 1048592
  397.6 1.4 fusion.2
  399.0 3.2 convolution_bitcast_fusion.1
  402.2 0.8 copy-done.3
  403.1 65.7 %psum.21 = f32[3]{0:T(128)S(1)} all-reduce(f32[3]{0:T(128)S(1)} %reduce_sum.48), channel_id=1, replica_groups=mesh['replica'=16,'data'=8] {'replica','data'}, use_global_device_ids=true, to_apply=%region_3.0 | all-reduce | flops 3 | bytes 24 | tf_op jit(solution)/shard_map/psum | solution.py:141
  468.8 0.6 fusion.11
  470.0 98.5 %all-reduce.4.cloned.1.call-done = (f32[2048,1024]{0,1:T(8,128)}, f32[512,1024]{0,1:T(8,128)}) async-done(((f32[2048,1024]{0,1:T(8,128)}, f32[512,1024]{0,1:T(8,128)}), (f32[2048,1024]{0,1:T(8,128)}, f32[512,1024]{0,1:T(8,128)})) %all-reduce.4.cloned.1.call-update) | async-done | bytes 10485776 | tf_op jit(solution)/shard_map/psum | solution.py:141
  568.5 9.4 %copy.25 = f32[2048,1024]{1,0:T(8,128)} copy(f32[2048,1024]{0,1:T(8,128)} %get-tuple-element.21) | data formatting | bytes 16777216
  577.9 1.8 copy.26
  (23 shorter events, 0.8 us)
Async XLA Ops:
  7.2 1.2 copy-start
  7.2 6.0 %copy-start.2 = (bf16[256,512]{1,0:T(8,128)(2,1)S(1)}, bf16[256,512]{1,0:T(8,128)(2,1)}, u32[]{:S(2)}) copy-start(bf16[256,512]{1,0:T(8,128)(2,1)} %param.7) | copy-start | bytes 786436
  7.2 44.6 %all-gather.3.cloned.1.call-start = ((), (), s32[]{:S(2)}) async-start(), calls=%async_computation.2 | async-start | bytes 4718592 | tf_op jit(solution)/shard_map/all_gather | solution.py:128
  13.2 112.4 %all-gather.5.cloned.1.call-start = ((), (), s32[]{:S(2)}) async-start(), calls=%async_computation.3 | async-start | bytes 8912896 | tf_op jit(solution)/shard_map/all_gather | solution.py:126
  15.9 268.2 %reduce-scatter.5.cloned.1.call-start = ((), (), s32[]{:S(2)}) async-start(), calls=%async_computation.4 | async-start | bytes 9437184 | tf_op jit(solution)/shard_map/reduce_scatter | solution.py:134
  232.2 165.4 %reduce-scatter.7.cloned.1.call-start = ((), (), s32[]{:S(2)}) async-start(), calls=%async_computation.5 | async-start | bytes 17825792
  249.7 318.8 %all-reduce.4.cloned.1.call-start = ((), (), s32[]{:S(2)}) async-start(), calls=%async_computation.6 | async-start | bytes 20971520 | tf_op jit(solution)/shard_map/psum | solution.py:141
  402.2 0.8 copy-start.3
  568.5 9.4 %copy-start.1 = (f32[512,1024]{0,1:T(8,128)S(1)}, f32[512,1024]{0,1:T(8,128)}, u32[]{:S(2)}) copy-start(f32[512,1024]{0,1:T(8,128)} %get-tuple-element.22) | copy-start | bytes 6291460
Sparse Core Ops, SparseCore 0:
  13.3 38.4 all-gather.2
  54.5 71.0 all-gather.4
  232.3 51.8 reduce-scatter.4
  287.4 110.1 reduce-scatter.6
  403.3 165.1 all-reduce.3

commit v2 on v1

v2 whole, which is shorter than its diff:
```python
import functools

import jax
import jax.numpy as jnp
from jax import lax
from jax.experimental import pallas as pl
from jax.experimental.pallas import tpu as pltpu
from jax.sharding import PartitionSpec as P

F32 = jnp.float32
BF16 = jnp.bfloat16
TILE = 512
MESH = pl.DeviceIdType.MESH
VMEM_LIMIT = 67043328


def normalize(raw):
    return raw * lax.rsqrt(jnp.sum(raw * raw, axis=-1, keepdims=True))


def embed_rows(feat_x, w_proj):
    raw_emb = jnp.dot(feat_x, w_proj, preferred_element_type=F32)
    unit_emb, pull_back = jax.vjp(normalize, raw_emb)
    return unit_emb.astype(BF16), pull_back


class Place:
    def __init__(self):
        rep, dat = lax.axis_index("replica"), lax.axis_index("data")
        self.z, self.y = lax.div(rep, 4), lax.rem(rep, 4)
        self.x, self.c = lax.div(dat, 2), lax.rem(dat, 2)

    def at(self, x=None, y=None, z=None, c=None):
        x = self.x if x is None else lax.rem(x + 8, 4)
        y = self.y if y is None else lax.rem(y + 8, 4)
        z = self.z if z is None else lax.rem(z + 8, 4)
        c = self.c if c is None else c
        return (z * 4 + y, x * 2 + c)

    def partner(self):
        return self.at(c=1 - self.c)

    def near(self, v):
        return v + 1 - 2 * lax.rem(v, 2)

    def far(self, v):
        return v - 1 + 2 * lax.rem(v, 2)

    def image_group(self):
        return Group(self.x, lax.rem(lax.div(self.y + 1, 2), 2), self.at(x=self.x + 1), self.at(x=self.x - 1), self.at(y=self.near(self.y)))

    def text_group(self):
        return Group(self.z, lax.div(self.y, 2), self.at(z=self.z + 1), self.at(z=self.z - 1), self.at(y=self.far(self.y)))

    def peers(self):
        out = [self.partner()]
        for g in (self.image_group(), self.text_group()):
            out += [g.right, g.left, g.pair]
        return out


class Group:
    def __init__(self, pos, side, right, left, pair):
        self.pos, self.side, self.right, self.left, self.pair = pos, side, right, left, pair

    def slot(self, twin, step):
        side = 1 - self.side if twin else self.side
        return side * 4 + lax.rem(self.pos + step + 4, 4)


def greet(place):
    barrier = pltpu.get_barrier_semaphore()
    peers = place.peers()
    for dev in peers:
        pl.semaphore_signal(barrier, inc=1, device_id=dev, device_id_type=MESH)
    pl.semaphore_wait(barrier, len(peers))


class Wire:
    def __init__(self, send, recv):
        self.send, self.recv, self.open = send, recv, []

    def go(self, k, src, dst, dev):
        copy = pltpu.make_async_remote_copy(src_ref=src, dst_ref=dst, send_sem=self.send.at[k], recv_sem=self.recv.at[k], device_id=dev, device_id_type=MESH)
        copy.start()
        self.open.append(copy)

    def got(self, k, dst, dev):
        pltpu.make_async_remote_copy(src_ref=dst, dst_ref=dst, send_sem=self.send.at[k], recv_sem=self.recv.at[k], device_id=dev, device_id_type=MESH).wait_recv()

    def drain(self):
        for copy in self.open:
            copy.wait_send()
        self.open = []


GATHER_COPIES = 8
SCATTER_COPIES = 10


def gather_stages(g, wire, own, blk, half, seen=None):
    seen = seen or (lambda slot: None)
    s = g.slot

    def start():
        me = s(False, 0)
        wire.go(0, own, blk(me), g.right)
        wire.go(1, own, blk(me), g.left)
        wire.go(2, own, blk(me), g.pair)

    def ring():
        wire.got(0, blk(s(False, -1)), g.left)
        wire.go(3, half(s(False, -1), 0), half(s(False, -1), 0), g.right)
        wire.got(1, blk(s(False, 1)), g.right)
        wire.go(4, half(s(False, 1), 1), half(s(False, 1), 1), g.left)
        seen(s(False, -1))
        seen(s(False, 1))

    def twin():
        wire.got(2, blk(s(True, 0)), g.pair)
        wire.go(5, blk(s(True, 0)), blk(s(True, 0)), g.right)
        wire.go(6, blk(s(True, 0)), blk(s(True, 0)), g.left)
        seen(s(True, 0))

    def across():
        wire.got(3, half(s(False, 2), 0), g.left)
        wire.got(4, half(s(False, 2), 1), g.right)
        wire.go(7, blk(s(False, 2)), blk(s(False, 2)), g.pair)
        seen(s(False, 2))

    def last():
        wire.got(5, blk(s(True, -1)), g.left)
        wire.got(6, blk(s(True, 1)), g.right)
        seen(s(True, -1))
        seen(s(True, 1))
        wire.got(7, blk(s(True, 2)), g.pair)
        seen(s(True, 2))

    return [start, ring, twin, across, last]


def scatter_stages(g, wire, blk, half, bufs, done):
    whole, part = bufs
    s = g.slot
    rp, rr0, rr1, rf0, rf1, rf2 = (whole.at[k] for k in range(6))
    rh0, rh1 = part.at[0], part.at[1]
    rows = part.shape[1]
    lo, hi = pl.ds(0, rows), pl.ds(rows, rows)

    def start():
        wire.go(0, blk(s(True, 2)), rp, g.pair)
        wire.go(1, blk(s(True, 1)), rr0, g.right)
        wire.go(2, blk(s(True, -1)), rr1, g.left)
        wire.go(3, half(s(False, 1), 1), rf0.at[hi], g.right)
        wire.go(4, half(s(False, -1), 0), rf1.at[lo], g.left)

    def across():
        wire.got(0, rp, g.pair)
        for h, sl in ((0, lo), (1, hi)):
            v = half(s(False, 2), h)
            v[...] += rp[sl]
        wire.go(5, half(s(False, 2), 0), rh0, g.right)
        wire.go(6, half(s(False, 2), 1), rh1, g.left)

    def twin():
        wire.got(1, rr0, g.left)
        wire.got(2, rr1, g.right)
        v = blk(s(True, 0))
        v[...] += rr0[...] + rr1[...]
        wire.go(7, v, rf2, g.pair)

    def ring():
        wire.got(5, rh0, g.left)
        v = half(s(False, 1), 0)
        v[...] += rh0[...]
        wire.go(8, v, rf0.at[lo], g.right)
        wire.got(6, rh1, g.right)
        v = half(s(False, -1), 1)
        v[...] += rh1[...]
        wire.go(9, v, rf1.at[hi], g.left)

    def last():
        wire.got(3, rf0.at[hi], g.left)
        wire.got(4, rf1.at[lo], g.right)
        wire.got(7, rf2, g.pair)
        wire.got(8, rf0.at[lo], g.left)
        wire.got(9, rf1.at[hi], g.right)
        done(rf0, rf1, rf2)

    return [start, across, twin, ring, last]


def run_both(a, b):
    for fa, fb in zip(a, b):
        fa()
        fb()


def rows_of(ref, size):
    def blk(slot):
        return ref.at[pl.ds(pl.multiple_of(slot * size, size), size)]

    def half(slot, h):
        return ref.at[pl.ds(pl.multiple_of(slot * size + h * (size // 2), size // 2), size // 2)]

    return blk, half


def score_terms(sim, scale, bias, diag):
    z = scale * sim + bias
    if diag is not None:
        z = jnp.where(diag, -z, z)
    e = jnp.exp(-jnp.abs(z))
    r = 1.0 / (1.0 + e)
    g = jnp.where(z >= 0.0, r, e * r)
    loss = jnp.maximum(z, 0.0) + jnp.log1p(e)
    if diag is not None:
        g = jnp.where(diag, -g, g)
    return loss, g


def fold(x):
    x = jnp.sum(x.reshape(x.shape[0] // 8, 8, x.shape[1]), axis=0)
    return sum(x[:, k * 128 : (k + 1) * 128] for k in range(x.shape[1] // 128))


def main_kernel(
    block, scal, img_own, txt_own, x_give, d_img_out, d_txt_out, sums, x_got,
    img, txt, d_img, d_txt, give, sbuf, gbuf,
    ibuf, ihalf, tbuf, thalf,
    ig_s, ig_r, tg_s, tg_r, is_s, is_r, ts_s, ts_r, core_s, core_r, local,
):
    place = Place()
    gi, gt = place.image_group(), place.text_group()
    c = place.c
    partner = place.partner()
    greet(place)

    half_rows = 8 * block
    img_blk, img_half = rows_of(img, block)
    core = Wire(core_s, core_r)
    core.go(0, x_give, x_got, partner)

    def txt_view(cc):
        def blk(slot):
            return txt.at[pl.ds(pl.multiple_of(cc * half_rows + slot * block, block), block)]

        def half(slot, h):
            return txt.at[pl.ds(pl.multiple_of(cc * half_rows + slot * block + h * (block // 2), block // 2), block // 2)]

        return blk, half

    txt_blk, txt_half = txt_view(c)
    other_blk, _ = txt_view(1 - c)
    wi, wt = Wire(ig_s, ig_r), Wire(tg_s, tg_r)

    counter = [1]

    def share(slot):
        core.go(counter[0], txt_blk(slot), txt_blk(slot), partner)
        counter[0] += 1

    core.go(counter[0], txt_own, txt_blk(gt.slot(False, 0)), partner)
    counter[0] += 1
    own_i = pltpu.make_async_copy(img_own, img_blk(gi.slot(False, 0)), local.at[0])
    own_t = pltpu.make_async_copy(txt_own, txt_blk(gt.slot(False, 0)), local.at[1])
    own_i.start()
    own_t.start()
    a = gather_stages(gi, wi, img_own, img_blk, img_half)
    b = gather_stages(gt, wt, txt_own, txt_blk, txt_half, share)
    a[0]()
    b[0]()
    d_img[...] = jnp.zeros_like(d_img)
    sums[...] = jnp.zeros_like(sums)
    run_both(a[1:], b[1:])
    own_i.wait()
    own_t.wait()
    order = [(False, 0), (False, -1), (False, 1), (True, 0), (False, 2), (True, -1), (True, 1), (True, 2)]
    for k, (twin, step) in enumerate(order):
        core.got(1 + k, other_blk(gt.slot(twin, step)), partner)
    core.got(0, x_got, partner)
    wi.drain()
    wt.drain()
    core.drain()

    scale, bias = scal[0], scal[1]
    chunks = half_rows // TILE
    per = TILE // block
    own_ci = lax.div(gi.slot(False, 0), per)
    own_ct = lax.div(gt.slot(False, 0), per)

    def img_rows(i):
        return pl.ds(pl.multiple_of(lax.rem(own_ci + i, chunks) * TILE, TILE), TILE)

    def chunk_of(k):
        return 2 * lax.rem(gt.side + lax.div(k + 1, 2), 2) + lax.rem(lax.rem(own_ct, 2) + lax.div(k, 2), 2)

    def txt_rows(cc, k):
        return pl.ds(pl.multiple_of(cc * half_rows + chunk_of(k) * TILE, TILE), TILE)

    count = chunks * chunks

    def sweep(cc, target, masked, enter, leave):
        def where(n):
            return lax.rem(n, chunks), lax.div(n, chunks)

        def score(n, slot):
            i, k = where(n)
            sbuf[slot] = lax.dot_general(img[img_rows(i), :], txt[txt_rows(cc, k), :], (((1,), (1,)), ((), ())), preferred_element_type=F32)

        def point(slot, diag=None):
            sim = sbuf[slot]
            loss, g = score_terms(sim, scale, bias, diag)
            sums[0] += fold(loss)
            sums[1] += fold(g * sim)
            sums[2] += fold(g)
            gbuf[slot] = g.astype(BF16)

        def products(n, slot):
            i, k = where(n)
            gb = gbuf[slot]
            rows = img_rows(i)
            d_img[rows, :] += jnp.dot(gb, txt[txt_rows(cc, k), :], preferred_element_type=F32)
            ref, at = target(k)
            ref[at, :] += lax.dot_general(gb, img[rows, :], (((0,), (0,)), ((), ())), preferred_element_type=F32)

        diag = None
        if masked:
            row = lax.broadcasted_iota(jnp.int32, (TILE, TILE), 0) - lax.rem(gi.slot(False, 0), per) * block
            col = lax.broadcasted_iota(jnp.int32, (TILE, TILE), 1) - lax.rem(gt.slot(False, 0), per) * block
            diag = (row == col) & (row >= 0) & (row < block)
        score(0, 0)
        score(1, 1)
        point(0, diag)
        per_k = chunks // 2

        def step(m, carry):
            n = 2 * m
            k = lax.div(m, per_k)

            @pl.when(lax.rem(m, per_k) == 0)
            def _():
                enter(k)

            score(n + 2, 0)
            point(1)
            products(n, 0)
            score(n + 3, 1)
            point(0)
            products(n + 1, 1)

            @pl.when(lax.rem(m, per_k) == per_k - 1)
            def _():
                leave(k)

            return carry

        lax.fori_loop(0, count // 2 - 1, step, 0)
        point(1)
        products(count - 2, 0)
        products(count - 1, 1)
        leave(chunks - 1)

    def give_rows(k):
        return pl.ds(pl.multiple_of(lax.rem(k, 2) * TILE, TILE), TILE)

    def d_rows(k):
        return pl.ds(pl.multiple_of(chunk_of(k) * TILE, TILE), TILE)

    base = 9

    def hand(k):
        return pltpu.make_async_remote_copy(
            src_ref=give.at[give_rows(k)], dst_ref=d_txt.at[d_rows(k)], send_sem=core_s.at[base + k], recv_sem=core_r.at[base + k], device_id=partner, device_id_type=MESH
        )

    def enter_give(k):
        @pl.when(k >= 2)
        def _():
            hand(k - 2).wait_send()

        give[give_rows(k), :] = jnp.zeros((TILE, give.shape[1]), F32)

    sweep(1 - c, lambda k: (give, give_rows(k)), False, enter_give, lambda k: hand(k).start())
    sweep(c, lambda k: (d_txt, d_rows(k)), True, lambda k: hand(k).wait_recv(), lambda k: None)
    hand(2).wait_send()
    hand(3).wait_send()

    wi, wt = Wire(is_s, is_r), Wire(ts_s, ts_r)
    di_blk, di_half = rows_of(d_img, block)
    dt_blk, dt_half = rows_of(d_txt, block)

    def finish(out, mine):
        def done(p, q, r):
            out[...] = (mine[...] + p[...]) + (q[...] + r[...])

        return done

    run_both(
        scatter_stages(gi, wi, di_blk, di_half, (ibuf, ihalf), finish(d_img_out, di_blk(gi.slot(False, 0)))),
        scatter_stages(gt, wt, dt_blk, dt_half, (tbuf, thalf), finish(d_txt_out, dt_blk(gt.slot(False, 0)))),
    )
    wi.drain()
    wt.drain()


def main_call(scal, img_emb, txt_emb, x_give):
    block, dim = img_emb.shape
    vmem = pl.BlockSpec(memory_space=pltpu.VMEM)
    hbm = pl.BlockSpec(memory_space=pl.ANY)
    sem = pltpu.SemaphoreType.DMA
    f = lambda *s: pltpu.VMEM(s, F32)
    return pl.pallas_call(
        functools.partial(main_kernel, block),
        in_specs=[pl.BlockSpec(memory_space=pltpu.SMEM), vmem, vmem, hbm],
        out_specs=[vmem, vmem, vmem, hbm],
        out_shape=[
            jax.ShapeDtypeStruct((block, dim), F32),
            jax.ShapeDtypeStruct((block, dim), F32),
            jax.ShapeDtypeStruct((3, 8, 128), F32),
            jax.ShapeDtypeStruct(x_give.shape, x_give.dtype),
        ],
        scratch_shapes=[
            pltpu.VMEM((8 * block, dim), BF16),
            pltpu.VMEM((16 * block, dim), BF16),
            f(8 * block, dim),
            f(8 * block, dim),
            f(2 * TILE, dim),
            f(2, TILE, TILE),
            pltpu.VMEM((2, TILE, TILE), BF16),
            f(6, block, dim),
            f(2, block // 2, dim),
            f(6, block, dim),
            f(2, block // 2, dim),
            sem((GATHER_COPIES,)), sem((GATHER_COPIES,)), sem((GATHER_COPIES,)), sem((GATHER_COPIES,)),
            sem((SCATTER_COPIES,)), sem((SCATTER_COPIES,)), sem((SCATTER_COPIES,)), sem((SCATTER_COPIES,)),
            sem((13,)), sem((13,)), sem((2,)),
        ],
        compiler_params=pltpu.CompilerParams(collective_id=0, has_side_effects=True, vmem_limit_bytes=VMEM_LIMIT),
        name="scores",
    )(scal, img_emb, txt_emb, x_give)


def sum_kernel(
    x_own, x_got, du_own, sums_in, out, sums,
    w, du, abuf, ahalf, bbuf, bhalf, abuf2, ahalf2, bbuf2, bhalf2, small,
    du_s, du_r, a1s, a1r, b1s, b1r, a2s, a2r, b2s, b2r, a3s, a3r, b3s, b3r, a4s, a4r, b4s, b4r, d_s, d_r, q_s, q_r,
):
    place = Place()
    gi, gt = place.image_group(), place.text_group()
    c = place.c
    partner = place.partner()
    greet(place)
    block = du_own.shape[1]
    img_f = (w.shape[0] // 5) * 4
    pre = Wire(du_s, du_r)
    pre.go(0, du_own, du, partner)

    def outer(lhs, rhs):
        return lax.dot_general(lhs, rhs, (((0,), (0,)), ((), ())), preferred_element_type=F32)

    w[:img_f] = outer(x_own[:, :img_f], du_own[0])
    w[img_f:] = outer(x_own[:, img_f:], du_own[1])
    pre.got(0, du, partner)
    w[:img_f] += outer(x_got[:, :img_f], du[0])
    w[img_f:] += outer(x_got[:, img_f:], du[1])
    pre.drain()

    small_wire = Wire(q_s, q_r)
    hops = [
        place.at(x=place.near(place.x)), place.at(x=place.far(place.x)), place.at(y=place.near(place.y)), place.at(y=place.far(place.y)),
        place.at(z=place.near(place.z)), place.at(z=place.far(place.z)), partner,
    ]
    small[0] = sums_in[...]

    def small_send(k):
        small_wire.go(k, small.at[2 * k], small.at[2 * k + 1], hops[k])

    def small_take(k):
        small_wire.got(k, small.at[2 * k + 1], hops[k])
        small[2 * k + 2] = small[2 * k] + small[2 * k + 1]

    rows = w.shape[0] // 16
    lanes = w.shape[1] // 8

    def colour(n, g1, g2, s1, s2, s3, s4, buf1, half1, buf2, half2):
        base = n * 8 * rows
        mine = base + g1.slot(False, 0) * rows

        def view(ref):
            def blk(slot):
                return ref.at[pl.ds(pl.multiple_of(base + slot * rows, rows), rows)]

            def half(slot, h):
                return ref.at[pl.ds(pl.multiple_of(base + slot * rows + h * (rows // 2), rows // 2), rows // 2)]

            return blk, half

        def strip(ref):
            def blk(slot):
                return ref.at[pl.ds(pl.multiple_of(mine, rows), rows), pl.ds(pl.multiple_of(slot * lanes, lanes), lanes)]

            def half(slot, h):
                return ref.at[pl.ds(pl.multiple_of(mine + h * (rows // 2), rows // 2), rows // 2), pl.ds(pl.multiple_of(slot * lanes, lanes), lanes)]

            return blk, half

        wires = [Wire(*s) for s in (s1, s2, s3, s4)]
        w_blk, w_half = view(w)
        ws_blk, ws_half = strip(w)
        o_blk, o_half = view(out.at[c])
        os_blk, os_half = strip(out.at[c])

        def done1(p, q, r):
            v = w_blk(g1.slot(False, 0))
            v[...] += p[...] + q[...] + r[...]

        def done2(p, q, r):
            me = g2.slot(False, 0)
            v = os_blk(me)
            v[...] = ws_blk(me)[...] + p[...] + q[...] + r[...]

        me2 = g2.slot(False, 0)
        count = [n * 8]

        def share(slot):
            dwire.go(count[0], o_blk(slot), o_blk(slot), partner)
            count[0] += 1

        def share_own():
            share(g1.slot(False, 0))

        stages = scatter_stages(g1, wires[0], w_blk, w_half, (buf1, half1), done1)
        stages += scatter_stages(g2, wires[1], ws_blk, ws_half, (buf2, half2), done2)
        stages += gather_stages(g2, wires[2], os_blk(me2), os_blk, os_half)
        tail = gather_stages(g1, wires[3], o_blk(g1.slot(False, 0)), o_blk, o_half, share)
        stages += [tail[0], share_own] + tail[1:]
        return stages, wires

    dwire = Wire(d_s, d_r)
    sa, wa = colour(0, gi, gt, (a1s, a1r), (a2s, a2r), (a3s, a3r), (a4s, a4r), abuf, ahalf, abuf2, ahalf2)
    sb, wb = colour(1, gt, gi, (b1s, b1r), (b2s, b2r), (b3s, b3r), (b4s, b4r), bbuf, bhalf, bbuf2, bhalf2)
    for n, (fa, fb) in enumerate(zip(sa, sb)):
        fa()
        fb()
        if n < 8:
            if n > 0:
                small_take(n - 1)
            if n < 7:
                small_send(n)
    sums[...] = small[14]
    order = [(False, 0), (False, -1), (False, 1), (True, 0), (False, 2), (True, -1), (True, 1), (True, 2)]
    for n, g1 in ((0, gi), (1, gt)):
        for k, (twin, step) in enumerate(order):
            v = out.at[1 - c].at[pl.ds(pl.multiple_of(n * 8 * rows + g1.slot(twin, step) * rows, rows), rows)]
            dwire.got(n * 8 + k, v, partner)
    for wire in wa + wb + [dwire, small_wire]:
        wire.drain()


def sum_call(x_own, x_got, du, sums):
    block, feats = x_own.shape
    dim = du.shape[2]
    vmem = pl.BlockSpec(memory_space=pltpu.VMEM)
    sem = pltpu.SemaphoreType.DMA
    f = lambda *s: pltpu.VMEM(s, F32)
    rows, lanes = feats // 16, dim // 8
    sc, ga = sem((SCATTER_COPIES,)), sem((GATHER_COPIES,))
    return pl.pallas_call(
        sum_kernel,
        in_specs=[vmem] * 4,
        out_specs=[vmem, vmem],
        out_shape=[jax.ShapeDtypeStruct((2, feats, dim), F32), jax.ShapeDtypeStruct(sums.shape, F32)],
        scratch_shapes=[
            f(feats, dim),
            pltpu.VMEM(du.shape, BF16),
            f(6, rows, dim), f(2, rows // 2, dim), f(6, rows, dim), f(2, rows // 2, dim),
            f(6, rows, lanes), f(2, rows // 2, lanes), f(6, rows, lanes), f(2, rows // 2, lanes),
            f(15, *sums.shape),
            sem((1,)), sem((1,)),
            sc, sc, sc, sc, sc, sc, sc, sc,
            ga, ga, ga, ga, ga, ga, ga, ga,
            sem((16,)), sem((16,)), sem((7,)), sem((7,)),
        ],
        compiler_params=pltpu.CompilerParams(collective_id=1, has_side_effects=True, vmem_limit_bytes=VMEM_LIMIT),
        name="weights",
    )(x_own, x_got, du, sums)


def solution(mesh):
    dev_count = mesh.shape["replica"] * mesh.shape["data"]
    batch_axes = ("replica", "data")

    def local_fn(img_x, txt_x, w_img, w_txt, log_temp, logit_bias):
        block = img_x.shape[0]
        total_rows = block * dev_count
        img_f, txt_f = img_x.shape[1] // 2, txt_x.shape[1] // 2
        core = lax.rem(lax.axis_index("data"), 2)

        def halves(which):
            a = lax.dynamic_slice_in_dim(img_x, which * img_f, img_f, axis=1)
            b = lax.dynamic_slice_in_dim(txt_x, which * txt_f, txt_f, axis=1)
            return jnp.concatenate([a, b], axis=1)

        txt_emb, txt_pull = embed_rows(txt_x, w_txt)
        img_emb, img_pull = embed_rows(img_x, w_img)
        temp_scale = jnp.exp(log_temp[0])
        scal = jnp.stack([temp_scale, logit_bias[0]])
        d_img, d_txt, sums, x_got = main_call(scal, img_emb, txt_emb, halves(1 - core))
        post = temp_scale / total_rows
        d_img_raw = img_pull(post * d_img)[0].astype(BF16)
        d_txt_raw = txt_pull(post * d_txt)[0].astype(BF16)
        grads, sums = sum_call(halves(core), x_got, jnp.stack([d_img_raw, d_txt_raw]), sums)
        d_w_img = grads[:, :img_f].reshape(2 * img_f, -1)
        d_w_txt = grads[:, img_f:].reshape(2 * txt_f, -1)
        parts = jnp.sum(sums, axis=(1, 2)) / total_rows
        return parts[0:1], temp_scale * parts[1:2], parts[2:3], d_w_img, d_w_txt

    batch_spec = P(batch_axes, None)
    return jax.shard_map(local_fn, mesh=mesh, in_specs=(batch_spec, batch_spec, P(), P(), P(), P()), out_specs=(P(), P(), P(), P(), P()), check_vma=False)
```

time: 588 us -> 291 us (0.49)
  waiting for transfers between devices: 340 us -> 0 us
  Pallas kernels: 97.5 us -> 260 us
  blocking collectives: 65.7 us -> 0 us
  local copies, waits for them, and re-layouts: 47.1 us -> 17 us
  between operations: 17 us -> 3.98 us
  matrix products: 14.3 us -> 1.87 us
    pallas_call x1 -> x2, Pallas kernels: 97.5 us -> 260 us  [the longest x1 178 us: main_call(): pl.pallas_call(functools.partial(main_kernel, block), in_specs=[pl.BlockS...]
    unnamed x6 -> x0, waiting for transfers between devices: 106 us -> none
    all_gather x2 -> x0, waiting for transfers between devices: 101 us -> none  [the longest x1 67.4 us: local_fn(): txt_all = lax.all_gather(txt_emb, 'replica', axis=0, tiled=True)]
    psum x1 -> x0, waiting for transfers between devices: 98.5 us -> none  [local_fn(): parts, d_w_img, d_w_txt = lax.psum((parts, d_w_img, d_w_txt), batch_axes)]
    psum x1 -> x0, blocking collectives: 65.7 us -> none  [local_fn(): parts, d_w_img, d_w_txt = lax.psum((parts, d_w_img, d_w_txt), batch_axes)]
    reduce_scatter x1 -> x0, waiting for transfers between devices: 34.4 us -> none  [local_fn(): d_img = lax.psum_scatter(d_img, 'data', scatter_dimension=0, tiled=True)]
    reshape x1 -> x0, local copies, waits for them, and re-layouts: 17.5 us -> none  [local_fn(): d_txt = d_txt.reshape(dim, rep_count, block).transpose(1, 0, 2)]
    slice x0 -> x2, local copies, waits for them, and re-layouts: none -> 11.6 us  [the longest x1 8.44 us: local_fn(): d_w_img = grads[:, :img_f].reshape(2 * img_f, -1)]
  transfers between devices with their start and end apart: 5 -> 0, of which waited for: 5 -> 0; matrix products, arithmetic and copies ran while one was open for 6% -> 0% of each run, Pallas kernels for 0% -> 0%
where the time goes in v2:
time: 291 us; the launch traced here: 290 us
  Pallas kernels  260 us (89%)
  local copies, waits for them, and re-layouts  17 us (6%)
  other arithmetic  7.32 us (3%)
  between operations  3.98 us (1%)
    pallas_call x1, Pallas kernels, main_call(): pl.pallas_call(functools.partial(main_kernel, block), in_specs=[pl.BlockS...  178 us
    pallas_call x1, Pallas kernels, sum_call(): pl.pallas_call(sum_kernel, in_specs=[vmem] * 4, out_specs=[vmem, vmem], o...  82.1 us
    slice x1, local copies, waits for them, and re-layouts, local_fn(): d_w_img = grads[:, :img_f].reshape(2 * img_f, -1)  8.44 us

profile of v2, /device:TPU:1, one launch (start us, length us, event | category | flops | bytes accessed | tf_op | source)
XLA Modules:
  0.0 290.3 jit_solution(14375386606642415463)
XLA Ops:
  2.0 0.6 pad_maximum_fusion.3.scal
  2.6 1.1 constant_dynamic-slice_fusion
  3.7 0.0 copy-start.8
  3.7 1.5 constant_dynamic-slice_fusion.1
  5.2 1.1 pad_maximum_fusion.1
  6.4 1.3 multiply_reduce_fusion.3
  7.8 0.6 copy-done.15
  8.3 0.5 multiply_reduce_fusion.2
  8.9 0.9 copy-done
  9.9 1.1 multiply_convert_fusion
  11.0 178.0 %scores.1 = (f32[256,1024]{1,0:T(8,128)}, f32[256,1024]{1,0:T(8,128)}, f32[3,8,128]{2,1,0:T(8,128)}, bf16[256,1280]{1,0:T(8,128)(2,1)}) custom-call(f32[2]{0:T(128)} %pad_maximum_fusion.3.scal, bf16[256,1024]{1,0:T(8,128)(2,1)} %get-tuple-element.31.img_own, bf16[256,1024]{1,0:T(8,128)(2,1)} %get-tuple-element.30.txt_own, ...), custom_call_target="tpu_custom_call" | custom-call | tf_op jit(solution)/shard_map/scores/pallas_call | solution.py:413
  189.1 1.9 multiply_reduce_fusion.1
  191.0 0.2 copy-done.5
  191.2 0.2 fusion.3
  191.5 0.1 copy-done.1
  191.5 0.3 copy-done.4
  191.9 0.2 multiply_reduce_fusion
  192.1 0.2 fusion.2
  192.3 1.1 pad_maximum_fusion.du_own
  193.4 82.1 %weights.1 = (f32[2,1280,1024]{2,1,0:T(8,128)}, f32[3,8,128]{2,1,0:T(8,128)}) custom-call(bf16[256,1280]{1,0:T(8,128)(2,1)} %get-tuple-element.28.x_own, bf16[256,1280]{1,0:T(8,128)(2,1)} %get-tuple-element.11.x_got, bf16[2,256,1024]{2,1,0:T(8,128)(2,1)} %pad_maximum_fusion.du_own, f32[3,8,128]{2,1,0:T(8,128)} %get-tuple-element.14.sums_in), custom_call_target="tpu_custom_call" | custom-call | tf_op jit(solution)/shard_map/weights/pallas_call | solution.py:569
  275.5 0.8 reduce_sum.57
  276.3 0.6 fusion.4
  277.6 3.2 %slice.19 = f32[2,256,1024]{2,1,0:T(8,128)} slice(f32[2,1280,1024]{2,1,0:T(8,128)} %get-tuple-element.16), slice={[0:2], [1024:1280], [0:1024]} | slice | bytes 4194304 | tf_op jit(solution)/shard_map/slice | solution.py:615
  280.8 8.4 %slice.18 = f32[2,1024,1024]{2,1,0:T(8,128)} slice(f32[2,1280,1024]{2,1,0:T(8,128)} %get-tuple-element.16), slice={[0:2], [0:1024], [0:1024]} | slice | bytes 16777216 | tf_op jit(solution)/shard_map/slice | solution.py:614
  (35 shorter events, 0.1 us)
Async XLA Ops:
  2.6 3.8 %copy-start.17 = (bf16[2048,1024]{1,0:T(8,128)(2,1)S(1)}, bf16[2048,1024]{1,0:T(8,128)(2,1)}, u32[]{:S(2)}) copy-start(bf16[2048,1024]{1,0:T(8,128)(2,1)} %param.8) | copy-start | bytes 12582916
  3.7 2.7 copy-start.8
  6.4 1.9 copy-start.6
  6.4 1.9 copy-start.7
  7.7 0.6 copy-start.15
  7.8 3.2 %copy-start.2 = (f32[256,1024]{1,0:T(8,128)}, f32[256,1024]{1,0:T(8,128)S(1)}, u32[]{:S(2)}) copy-start(f32[256,1024]{1,0:T(8,128)S(1)} %get-tuple-element.25) | copy-start | bytes 3145732
  8.3 2.7 copy-start.11
  8.9 1.0 copy-start
  8.9 2.1 copy-start.13
  9.8 1.2 copy-start.9
  189.0 1.9 copy-start.16
  189.0 2.0 copy-start.3
  189.1 2.2 copy-start.5
  189.1 2.2 copy-start.12
  189.1 2.5 copy-start.1
  189.1 2.8 copy-start.4
  191.2 0.8 copy-start.14
  191.2 0.8 copy-start.10

commit v3 on v1

v3 whole, which is shorter than its diff:
```python
import functools

import jax
import jax.numpy as jnp
from jax import lax
from jax.experimental import pallas as pl
from jax.experimental.pallas import tpu as pltpu
from jax.sharding import PartitionSpec as P

F32 = jnp.float32
BF16 = jnp.bfloat16
TILE = 512
MESH = pl.DeviceIdType.MESH
VMEM_LIMIT = 67043328


def normalize(raw):
    return raw * lax.rsqrt(jnp.sum(raw * raw, axis=-1, keepdims=True))


def embed_rows(feat_x, w_proj):
    raw_emb = jnp.dot(feat_x, w_proj, preferred_element_type=F32)
    unit_emb, pull_back = jax.vjp(normalize, raw_emb)
    return unit_emb.astype(BF16), pull_back


class Place:
    def __init__(self):
        rep, dat = lax.axis_index("replica"), lax.axis_index("data")
        self.z, self.y = lax.div(rep, 4), lax.rem(rep, 4)
        self.x, self.c = lax.div(dat, 2), lax.rem(dat, 2)

    def at(self, x=None, y=None, z=None, c=None):
        x = self.x if x is None else lax.rem(x + 8, 4)
        y = self.y if y is None else lax.rem(y + 8, 4)
        z = self.z if z is None else lax.rem(z + 8, 4)
        c = self.c if c is None else c
        return (z * 4 + y, x * 2 + c)

    def partner(self):
        return self.at(c=1 - self.c)

    def near(self, v):
        return v + 1 - 2 * lax.rem(v, 2)

    def far(self, v):
        return v - 1 + 2 * lax.rem(v, 2)

    def image_group(self):
        return Group(self.x, lax.rem(lax.div(self.y + 1, 2), 2), self.at(x=self.x + 1), self.at(x=self.x - 1), self.at(y=self.near(self.y)))

    def text_group(self):
        return Group(self.z, lax.div(self.y, 2), self.at(z=self.z + 1), self.at(z=self.z - 1), self.at(y=self.far(self.y)))

    def peers(self):
        out = [self.partner()]
        for g in (self.image_group(), self.text_group()):
            out += [g.right, g.left, g.pair]
        return out


class Group:
    def __init__(self, pos, side, right, left, pair):
        self.pos, self.side, self.right, self.left, self.pair = pos, side, right, left, pair

    def slot(self, key):
        side = 1 - self.side if key[0] else self.side
        return side * 4 + lax.rem(self.pos + key[1] + 4, 4)


def greet(place):
    barrier = pltpu.get_barrier_semaphore()
    peers = place.peers()
    for dev in peers:
        pl.semaphore_signal(barrier, inc=1, device_id=dev, device_id_type=MESH)
    pl.semaphore_wait(barrier, len(peers))


class Wire:
    def __init__(self, send, recv):
        self.send, self.recv, self.open = send, recv, []

    def copy(self, k, src, dst, dev):
        return pltpu.make_async_remote_copy(src_ref=src, dst_ref=dst, send_sem=self.send.at[k], recv_sem=self.recv.at[k], device_id=dev, device_id_type=MESH)

    def go(self, *what):
        self.copy(*what).start()
        self.open.append(what)

    def got(self, k, dst, dev):
        self.copy(k, dst, dst, dev).wait_recv()

    def drain(self):
        for what in self.open:
            self.copy(*what).wait_send()
        self.open = []


class Pieces:
    def __init__(self, send, recv):
        self.wire = Wire(send, recv)

    def go(self, k, src, dst, dev):
        for p in range(2):
            self.wire.go(2 * k + p, src[p], dst[p], dev)

    def got(self, k, dst, dev):
        for p in range(2):
            self.wire.got(2 * k + p, dst[p], dev)

    def drain(self):
        self.wire.drain()


GATHER_COPIES = 8
SCATTER_COPIES = 10


def gather_stages(wire, g, own, blk, half, relative, seen=None):
    seen = seen or (lambda key: None)

    def moved(key, way):
        twin, step = key
        if not relative:
            return key
        return {"right": (twin, step - 1), "left": (twin, step + 1), "pair": (not twin, step)}[way]

    def send(k, key, way, h=None):
        dev = getattr(g, way)
        view = blk if h is None else functools.partial(half, h=h)
        wire.go(k, view(key), view(moved(key, way)), dev)

    def start():
        for k, way in enumerate(("right", "left", "pair")):
            wire.go(k, own, blk(moved((False, 0), way)), getattr(g, way))

    def ring():
        wire.got(0, blk((False, -1)), g.left)
        send(3, (False, -1), "right", 0)
        wire.got(1, blk((False, 1)), g.right)
        send(4, (False, 1), "left", 1)
        seen((False, -1))
        seen((False, 1))

    def twin():
        wire.got(2, blk((True, 0)), g.pair)
        send(5, (True, 0), "right")
        send(6, (True, 0), "left")
        seen((True, 0))

    def across():
        wire.got(3, half((False, 2), 0), g.left)
        wire.got(4, half((False, 2), 1), g.right)
        send(7, (False, 2), "pair")
        seen((False, 2))

    def last():
        wire.got(5, blk((True, -1)), g.left)
        wire.got(6, blk((True, 1)), g.right)
        seen((True, -1))
        seen((True, 1))
        wire.got(7, blk((True, 2)), g.pair)
        seen((True, 2))

    return [start, ring, twin, across, last]


SEEN = [(False, 0), (False, -1), (False, 1), (True, 0), (False, 2), (True, -1), (True, 1), (True, 2)]


class Scatter:
    def __init__(self, wire, g, blk, half, bufs, finish):
        self.wire, self.g, self.blk, self.half, self.finish = wire, g, blk, half, finish
        whole, part = bufs
        self.rp, self.rr0, self.rr1, self.rf0, self.rf1, self.rf2 = (whole.at[k] for k in range(6))
        self.rh0, self.rh1 = part.at[0], part.at[1]
        rows = part.shape[1]
        self.lo, self.hi = pl.ds(0, rows), pl.ds(rows, rows)

    def twins(self):
        self.wire.go(1, self.blk((True, 1)), self.rr0, self.g.right)
        self.wire.go(2, self.blk((True, -1)), self.rr1, self.g.left)

    def opposite(self):
        self.wire.go(0, self.blk((True, 2)), self.rp, self.g.pair)

    def early(self):
        self.wire.go(3, self.half((False, 1), 1), self.rf0.at[self.hi], self.g.right)
        self.wire.go(4, self.half((False, -1), 0), self.rf1.at[self.lo], self.g.left)

    def across(self):
        self.wire.got(0, self.rp, self.g.pair)
        for h, sl in ((0, self.lo), (1, self.hi)):
            v = self.half((False, 2), h)
            v[...] += self.rp[sl]
        self.wire.go(5, self.half((False, 2), 0), self.rh0, self.g.right)
        self.wire.go(6, self.half((False, 2), 1), self.rh1, self.g.left)

    def twin(self):
        self.wire.got(1, self.rr0, self.g.left)
        self.wire.got(2, self.rr1, self.g.right)
        v = self.blk((True, 0))
        v[...] += self.rr0[...] + self.rr1[...]
        self.wire.go(7, v, self.rf2, self.g.pair)

    def ring(self):
        self.wire.got(5, self.rh0, self.g.left)
        v = self.half((False, 1), 0)
        v[...] += self.rh0[...]
        self.wire.go(8, v, self.rf0.at[self.lo], self.g.right)
        self.wire.got(6, self.rh1, self.g.right)
        v = self.half((False, -1), 1)
        v[...] += self.rh1[...]
        self.wire.go(9, v, self.rf1.at[self.hi], self.g.left)

    def last(self):
        self.wire.got(3, self.rf0.at[self.hi], self.g.left)
        self.wire.got(4, self.rf1.at[self.lo], self.g.right)
        self.wire.got(7, self.rf2, self.g.pair)
        self.wire.got(8, self.rf0.at[self.lo], self.g.left)
        self.wire.got(9, self.rf1.at[self.hi], self.g.right)
        self.finish(self.rf0, self.rf1, self.rf2)

    def stages(self):
        def start():
            self.opposite()
            self.twins()
            self.early()

        return [start, self.across, self.twin, self.ring, self.last]


def run_both(a, b):
    for fa, fb in zip(a, b):
        fa()
        fb()


PLACE = {(False, 0): 0, (True, 0): 1, (False, 1): 2, (False, 3): 3, (True, 2): 4, (False, 2): 5, (True, 1): 6, (True, 3): 7}


def rows_of(ref, size, base=0):
    def at(key):
        return base + PLACE[key[0], key[1] % 4] * size

    def blk(key):
        return ref.at[pl.ds(at(key), size)]

    def half(key, h):
        return ref.at[pl.ds(at(key) + h * (size // 2), size // 2)]

    return blk, half


def score_terms(sim, scale, bias, diag):
    z = scale * sim + bias
    if diag is not None:
        z = jnp.where(diag, -z, z)
    e = jnp.exp(-jnp.abs(z))
    r = 1.0 / (1.0 + e)
    g = jnp.where(z >= 0.0, r, e * r)
    loss = jnp.maximum(z, 0.0) + jnp.log1p(e)
    if diag is not None:
        g = jnp.where(diag, -g, g)
    return loss, g


def fold(x):
    x = jnp.sum(x.reshape(x.shape[0] // 8, 8, x.shape[1]), axis=0)
    return sum(x[:, k * 128 : (k + 1) * 128] for k in range(x.shape[1] // 128))


def tile_of(m):
    div, least = (lambda a, b: a // b, min) if isinstance(m, int) else (lax.div, jnp.minimum)
    q = 3 - least(div(m, 7), 1) - least(div(m, 12), 1) - div(m, 15)
    r = m - (16 - (q + 1) * (q + 1))
    down = least(div(r, q + 1), 1)
    return q + down * (r - q - 1 - q), r + down * (q - r)


def main_kernel(
    block, scal, img_own, txt_own, img_x, txt_x, d_img_out, d_txt_out, sums, x_got,
    img, txt, d_img, d_txt, give, taken, sbuf, gbuf,
    ibuf, ihalf, tbuf, thalf,
    ig_s, ig_r, tg_s, tg_r, is_s, is_r, ts_s, ts_r, core_s, core_r, hand_s, hand_r, local, free,
):
    place = Place()
    gi, gt = place.image_group(), place.text_group()
    c = place.c
    partner = place.partner()
    greet(place)

    half_rows = 8 * block
    img_blk, img_half = rows_of(img, block)
    txt_blk, txt_half = rows_of(txt, block, half_rows)
    other_blk, _ = rows_of(txt, block)
    wi, wt, core = Wire(ig_s, ig_r), Wire(tg_s, tg_r), Wire(core_s, core_r)

    own_i = pltpu.make_async_copy(img_own, img_blk((False, 0)), local.at[0])
    own_t = pltpu.make_async_copy(txt_own, txt_blk((False, 0)), local.at[1])
    own_i.start()
    own_t.start()
    own_i.wait()
    own_t.wait()
    sent = iter(range(8))

    def share(key):
        core.go(next(sent), txt_blk(key), other_blk(key), partner)

    a = gather_stages(wi, gi, img_blk((False, 0)), img_blk, img_half, True)
    b = gather_stages(wt, gt, txt_blk((False, 0)), txt_blk, txt_half, True, share)
    a[0]()
    b[0]()
    share((False, 0))
    img_f, txt_f = img_x.shape[1] // 2, txt_x.shape[1] // 2
    core.go(8, img_x.at[:, pl.ds(pl.multiple_of((1 - c) * img_f, img_f), img_f)], x_got.at[:, pl.ds(0, img_f)], partner)
    core.go(9, txt_x.at[:, pl.ds(pl.multiple_of((1 - c) * txt_f, txt_f), txt_f)], x_got.at[:, pl.ds(img_f, txt_f)], partner)
    for ref in (d_img, d_txt, give, sums):
        ref[...] = jnp.zeros_like(ref)
    run_both(a[1:], b[1:])
    for k, key in enumerate(SEEN):
        core.got(k, other_blk(key), partner)
    core.got(8, x_got.at[:, pl.ds(0, img_f)], partner)
    core.got(9, x_got.at[:, pl.ds(img_f, txt_f)], partner)
    for wire in (wi, wt, core):
        wire.drain()

    scale, bias = scal[0], scal[1]
    di_blk, di_half = rows_of(d_img, block)
    dt_blk, dt_half = rows_of(d_txt, block)

    outs = []

    def finish(out, mine, k):
        def done(p, q, r):
            mine[...] += p[...] + (q[...] + r[...])
            copy = pltpu.make_async_copy(mine, out, local.at[k])
            copy.start()
            outs.append(copy)

        return done

    wi, wt = Wire(is_s, is_r), Wire(ts_s, ts_r)
    ri = Scatter(wi, gi, di_blk, di_half, (ibuf, ihalf), finish(d_img_out, di_blk((False, 0)), 0))
    rt = Scatter(wt, gt, dt_blk, dt_half, (tbuf, thalf), finish(d_txt_out, dt_blk((False, 0)), 1))

    def hand(k):
        return pltpu.make_async_remote_copy(
            src_ref=give.at[pl.ds(k * TILE, TILE)], dst_ref=taken.at[k % 2], send_sem=hand_s.at[k], recv_sem=hand_r.at[k], device_id=partner, device_id_type=MESH
        )

    def give_chunk(k):
        if k < 2:
            pl.semaphore_wait(free, 1)
        hand(k).start()

    def take_chunk(k):
        hand(k).wait_recv()
        v = d_txt.at[pl.ds(k * TILE, TILE)]
        v[...] += taken[k % 2]
        if k >= 2:
            pl.semaphore_signal(free, inc=1, device_id=partner, device_id_type=MESH)

    def rows(chunk, first=0):
        at = first + chunk * TILE
        return pl.ds(at if isinstance(at, int) else pl.multiple_of(at, TILE), TILE)

    def txt_rows(cc, chunk):
        return rows(chunk, cc * half_rows)

    def score(m, cc):
        i, j = tile_of(m)
        sbuf[cc] = lax.dot_general(img[rows(i), :], txt[txt_rows(cc, j), :], (((1,), (1,)), ((), ())), preferred_element_type=F32)

    def point(cc, diag=None):
        sim = sbuf[cc]
        loss, g = score_terms(sim, scale, bias, diag)
        sums[0] += fold(loss)
        sums[1] += fold(g * sim)
        sums[2] += fold(g)
        gbuf[cc] = g.astype(BF16)

    def products(m, cc):
        i, j = tile_of(m)
        gb = gbuf[cc]
        d_img[rows(i), :] += jnp.dot(gb, txt[txt_rows(cc, j), :], preferred_element_type=F32)
        ref = d_txt if cc else give
        ref[rows(j), :] += lax.dot_general(gb, img[rows(i), :], (((0,), (0,)), ((), ())), preferred_element_type=F32)

    events = {
        3: [ri.twins],
        6: [lambda: give_chunk(3)],
        7: [lambda: take_chunk(3), rt.twins],
        9: [ri.opposite],
        11: [lambda: give_chunk(2)],
        12: [lambda: take_chunk(2), rt.opposite],
        13: [ri.early],
        14: [lambda: give_chunk(1)],
    }
    score(0, 0)
    score(0, 1)
    point(0)

    def step(m, carry):
        score(m + 1, 0)
        point(1)
        products(m, 0)
        score(m + 1, 1)
        point(0)
        products(m, 1)
        for at, todo in events.items():
            @pl.when(m == at)
            def _(todo=todo):
                for f in todo:
                    f()

        return carry

    lax.fori_loop(0, 15, step, 0)
    row = lax.broadcasted_iota(jnp.int32, (TILE, TILE), 0)
    col = lax.broadcasted_iota(jnp.int32, (TILE, TILE), 1)
    point(1, (row == col) & (row < block))
    products(15, 0)
    give_chunk(0)
    products(15, 1)
    ri.across()
    take_chunk(1)
    rt.early()
    ri.twin()
    take_chunk(0)
    rt.twin()
    rt.across()
    ri.ring()
    rt.ring()
    ri.last()
    rt.last()
    for k in range(4):
        hand(k).wait_send()
    for copy in outs:
        copy.wait()
    wi.drain()
    wt.drain()


def main_call(scal, img_emb, txt_emb, img_x, txt_x):
    block, dim = img_emb.shape
    vmem = pl.BlockSpec(memory_space=pltpu.VMEM)
    hbm = pl.BlockSpec(memory_space=pl.ANY)
    sem = pltpu.SemaphoreType.DMA
    f = lambda *s: pltpu.VMEM(s, F32)
    return pl.pallas_call(
        functools.partial(main_kernel, block),
        in_specs=[pl.BlockSpec(memory_space=pltpu.SMEM), hbm, hbm, hbm, hbm],
        out_specs=[hbm, hbm, vmem, hbm],
        out_shape=[
            jax.ShapeDtypeStruct((block, dim), F32),
            jax.ShapeDtypeStruct((block, dim), F32),
            jax.ShapeDtypeStruct((3, 8, 128), F32),
            jax.ShapeDtypeStruct((block, (img_x.shape[1] + txt_x.shape[1]) // 2), BF16),
        ],
        scratch_shapes=[
            pltpu.VMEM((8 * block, dim), BF16),
            pltpu.VMEM((16 * block, dim), BF16),
            f(8 * block, dim),
            f(8 * block, dim),
            f(8 * block, dim),
            f(2, TILE, dim),
            f(2, TILE, TILE),
            pltpu.VMEM((2, TILE, TILE), BF16),
            f(6, block, dim),
            f(2, block // 2, dim),
            f(6, block, dim),
            f(2, block // 2, dim),
            sem((GATHER_COPIES,)), sem((GATHER_COPIES,)), sem((GATHER_COPIES,)), sem((GATHER_COPIES,)),
            sem((SCATTER_COPIES,)), sem((SCATTER_COPIES,)), sem((SCATTER_COPIES,)), sem((SCATTER_COPIES,)),
            sem((10,)), sem((10,)), sem((4,)), sem((4,)), sem((2,)), pltpu.SemaphoreType.REGULAR,
        ],
        compiler_params=pltpu.CompilerParams(collective_id=0, has_side_effects=True, vmem_limit_bytes=VMEM_LIMIT),
        name="scores",
    )(scal, img_emb, txt_emb, img_x, txt_x)


def sum_kernel(
    img_x, txt_x, x_got, du_own, sums_in, d_w_img, d_w_txt, sums,
    w, w2, du, abuf, ahalf, bbuf, bhalf, abuf2, ahalf2, bbuf2, bhalf2, small,
    du_s, du_r, a1s, a1r, b1s, b1r, a2s, a2r, b2s, b2r, a3s, a3r, b3s, b3r, a4s, a4r, b4s, b4r, d_s, d_r, q_s, q_r, local,
):
    place = Place()
    gi, gt = place.image_group(), place.text_group()
    c = place.c
    partner = place.partner()
    greet(place)
    img_f, txt_f = img_x.shape[1] // 2, txt_x.shape[1] // 2
    ni, nt = img_f // 16, txt_f // 16
    rows, lanes = ni + nt, w.shape[1] // 8
    pre = Wire(du_s, du_r)
    pre.go(0, du_own, du, partner)

    def outer(lhs, rhs):
        return lax.dot_general(lhs, rhs, (((0,), (0,)), ((), ())), preferred_element_type=F32)

    def weights(own, part):
        rhs = du_own if own else du
        for k in range(img_f // 128):
            cols = pl.ds(pl.multiple_of(c * img_f + k * 128, 128), 128)
            lhs = img_x[:, cols] if own else x_got[:, k * 128 : (k + 1) * 128]
            put(part, k * 128, 128, ni, 0, outer(lhs, rhs[0]), own)
        for k in range(txt_f // 128):
            cols = pl.ds(pl.multiple_of(c * txt_f + k * 128, 128), 128)
            lhs = txt_x[:, cols] if own else x_got[:, img_f + k * 128 : img_f + (k + 1) * 128]
            put(part, k * 128, 128, nt, ni, outer(lhs, rhs[1]), own)

    def put(ref, first, count, size, shift, val, fresh):
        for b in range(count // size):
            at = ((first + b * size) // size) * rows + shift
            piece = val[b * size : (b + 1) * size]
            if fresh:
                ref[at : at + size] = piece
            else:
                ref[at : at + size] += piece

    weights(True, w)
    pre.got(0, du, partner)
    weights(False, w)
    pre.drain()

    small_wire = Wire(q_s, q_r)
    hops = [
        place.at(x=place.near(place.x)), place.at(x=place.far(place.x)), place.at(y=place.near(place.y)), place.at(y=place.far(place.y)),
        place.at(z=place.near(place.z)), place.at(z=place.far(place.z)), partner,
    ]
    small[0] = sums_in[...]

    def small_send(k):
        small_wire.go(k, small.at[2 * k], small.at[2 * k + 1], hops[k])

    def small_take(k):
        small_wire.got(k, small.at[2 * k + 1], hops[k])
        small[2 * k + 2] = small[2 * k] + small[2 * k + 1]

    dwire = Pieces(d_s, d_r)
    copies = []

    def colour(n, g1, g2, s1, s2, s3, s4, buf1, half1, buf2, half2):
        base = n * 8 * rows
        mine = base + g1.slot((False, 0)) * rows

        def sl(first, count):
            return pl.ds(pl.multiple_of(first, count), count)

        def w_blk(key):
            return w.at[sl(base + g1.slot(key) * rows, rows)]

        def w_half(key, h):
            return w.at[sl(base + g1.slot(key) * rows + h * (rows // 2), rows // 2)]

        def strip(ref, first):
            def blk(key):
                return ref.at[sl(first, rows), sl(g2.slot(key) * lanes, lanes)]

            def half(key, h):
                return ref.at[sl(first + h * (rows // 2), rows // 2), sl(g2.slot(key) * lanes, lanes)]

            return blk, half

        def o_half(key, h):
            i0 = c * img_f + (n * 8 + g1.slot(key)) * ni
            t0 = c * txt_f + (n * 8 + g1.slot(key)) * nt
            return d_w_img.at[sl(i0 + h * (ni // 2), ni // 2)], d_w_txt.at[sl(t0 + h * (nt // 2), nt // 2)]

        def o_blk(key, core=c):
            i0 = core * img_f + (n * 8 + g1.slot(key)) * ni
            t0 = core * txt_f + (n * 8 + g1.slot(key)) * nt
            return d_w_img.at[sl(i0, ni)], d_w_txt.at[sl(t0, nt)]

        w1, wire2, w3 = Wire(*s1), Wire(*s2), Wire(*s3)
        w4 = Pieces(*s4)
        ws_blk, ws_half = strip(w, mine)
        os_blk, os_half = strip(w2, n * rows)
        home = (False, 0)

        def done1(p, q, r):
            v = w_blk(home)
            v[...] += p[...] + q[...] + r[...]

        def done2(p, q, r):
            v = os_blk(home)
            v[...] = ws_blk(home)[...] + p[...] + q[...] + r[...]

        count = [n * 8]
        whole = w2.at[n * rows : n * rows + ni], w2.at[n * rows + ni : (n + 1) * rows]

        def share(key, src=None):
            dwire.go(count[0], o_blk(key) if src is None else src, o_blk(key), partner)
            count[0] += 1

        def share_own():
            share(home, whole)
            for p, (src, dst) in enumerate(zip(whole, o_blk(home))):
                copy = pltpu.make_async_copy(src, dst, local.at[2 * n + p])
                copy.start()
                copies.append(copy)

        def got_shares():
            for k, key in enumerate(SEEN):
                dwire.got(n * 8 + k, o_blk(key, 1 - c), partner)

        stages = Scatter(w1, g1, w_blk, w_half, (buf1, half1), done1).stages()
        stages += Scatter(wire2, g2, ws_blk, ws_half, (buf2, half2), done2).stages()
        stages += gather_stages(w3, g2, os_blk(home), os_blk, os_half, False)
        tail = gather_stages(w4, g1, whole, o_blk, o_half, False, share)
        stages += [tail[0], share_own] + tail[1:] + [got_shares]
        return stages, [w1, wire2, w3, w4]

    sa, wa = colour(0, gi, gt, (a1s, a1r), (a2s, a2r), (a3s, a3r), (a4s, a4r), abuf, ahalf, abuf2, ahalf2)
    sb, wb = colour(1, gt, gi, (b1s, b1r), (b2s, b2r), (b3s, b3r), (b4s, b4r), bbuf, bhalf, bbuf2, bhalf2)
    for n, (fa, fb) in enumerate(zip(sa, sb)):
        fa()
        fb()
        if 0 < n < 8:
            small_take(n - 1)
        if n < 7:
            small_send(n)
    sums[...] = small[14]
    for copy in copies:
        copy.wait()
    for wire in wa + wb + [dwire, small_wire]:
        wire.drain()


def sum_call(img_x, txt_x, x_got, du, sums):
    block = img_x.shape[0]
    feats = x_got.shape[1]
    dim = du.shape[2]
    vmem = pl.BlockSpec(memory_space=pltpu.VMEM)
    hbm = pl.BlockSpec(memory_space=pl.ANY)
    sem = pltpu.SemaphoreType.DMA
    f = lambda *s: pltpu.VMEM(s, F32)
    rows, lanes = feats // 16, dim // 8
    sc, ga, ga2 = sem((SCATTER_COPIES,)), sem((GATHER_COPIES,)), sem((2 * GATHER_COPIES,))
    return pl.pallas_call(
        sum_kernel,
        in_specs=[vmem] * 5,
        out_specs=[hbm, hbm, vmem],
        out_shape=[
            jax.ShapeDtypeStruct((img_x.shape[1], dim), F32),
            jax.ShapeDtypeStruct((txt_x.shape[1], dim), F32),
            jax.ShapeDtypeStruct(sums.shape, F32),
        ],
        scratch_shapes=[
            f(feats, dim),
            f(2 * rows, dim),
            pltpu.VMEM(du.shape, BF16),
            f(6, rows, dim), f(2, rows // 2, dim), f(6, rows, dim), f(2, rows // 2, dim),
            f(6, rows, lanes), f(2, rows // 2, lanes), f(6, rows, lanes), f(2, rows // 2, lanes),
            f(15, *sums.shape),
            sem((1,)), sem((1,)),
            sc, sc, sc, sc, sc, sc, sc, sc,
            ga, ga, ga, ga, ga2, ga2, ga2, ga2,
            sem((32,)), sem((32,)), sem((7,)), sem((7,)), sem((4,)),
        ],
        compiler_params=pltpu.CompilerParams(collective_id=1, has_side_effects=True, vmem_limit_bytes=28 * 2**20),
        name="weights",
    )(img_x, txt_x, x_got, du, sums)


def solution(mesh):
    dev_count = mesh.shape["replica"] * mesh.shape["data"]
    batch_axes = ("replica", "data")

    def local_fn(img_x, txt_x, w_img, w_txt, log_temp, logit_bias):
        block = img_x.shape[0]
        total_rows = block * dev_count
        txt_emb, txt_pull = embed_rows(txt_x, w_txt)
        img_emb, img_pull = embed_rows(img_x, w_img)
        temp_scale = jnp.exp(log_temp[0])
        scal = jnp.stack([temp_scale, logit_bias[0]])
        d_img, d_txt, sums, x_got = main_call(scal, img_emb, txt_emb, img_x, txt_x)
        post = temp_scale / total_rows
        d_img_raw = img_pull(post * d_img)[0].astype(BF16)
        d_txt_raw = txt_pull(post * d_txt)[0].astype(BF16)
        d_w_img, d_w_txt, sums = sum_call(img_x, txt_x, x_got, jnp.stack([d_img_raw, d_txt_raw]), sums)
        parts = jnp.sum(sums, axis=(1, 2)) / total_rows
        return parts[0:1], temp_scale * parts[1:2], parts[2:3], d_w_img, d_w_txt

    batch_spec = P(batch_axes, None)
    return jax.shard_map(local_fn, mesh=mesh, in_specs=(batch_spec, batch_spec, P(), P(), P(), P()), out_specs=(P(), P(), P(), P(), P()), check_vma=False)
```

time: 588 us -> 270 us (0.46)
  waiting for transfers between devices: 340 us -> 0 us
  Pallas kernels: 97.5 us -> 239 us
  blocking collectives: 65.7 us -> 0 us
  local copies, waits for them, and re-layouts: 47.1 us -> 16.7 us
  between operations: 17 us -> 4 us
  matrix products: 14.3 us -> 4.46 us
    pallas_call x1 -> x2, Pallas kernels: 97.5 us -> 239 us  [the longest x1 161 us: main_call(): pl.pallas_call(functools.partial(main_kernel, block), in_specs=[pl.BlockS...]
    unnamed x6 -> x0, waiting for transfers between devices: 106 us -> none
    all_gather x2 -> x0, waiting for transfers between devices: 101 us -> none  [the longest x1 67.4 us: local_fn(): txt_all = lax.all_gather(txt_emb, 'replica', axis=0, tiled=True)]
    psum x1 -> x0, waiting for transfers between devices: 98.5 us -> none  [local_fn(): parts, d_w_img, d_w_txt = lax.psum((parts, d_w_img, d_w_txt), batch_axes)]
    psum x1 -> x0, blocking collectives: 65.7 us -> none  [local_fn(): parts, d_w_img, d_w_txt = lax.psum((parts, d_w_img, d_w_txt), batch_axes)]
    reduce_scatter x1 -> x0, waiting for transfers between devices: 34.4 us -> none  [local_fn(): d_img = lax.psum_scatter(d_img, 'data', scatter_dimension=0, tiled=True)]
    reshape x1 -> x0, local copies, waits for them, and re-layouts: 17.5 us -> none  [local_fn(): d_txt = d_txt.reshape(dim, rep_count, block).transpose(1, 0, 2)]
    pallas_call x1 -> x0, local copies, waits for them, and re-layouts: 9.11 us -> none  [tile_call(): pl.pallas_call(functools.partial(tile_kernel, block), grid=(cols // TILE,...]
  transfers between devices with their start and end apart: 5 -> 0, of which waited for: 5 -> 0; matrix products, arithmetic and copies ran while one was open for 6% -> 0% of each run, Pallas kernels for 0% -> 0%
where the time goes in v3:
time: 270 us; the launch traced here: 269 us
  Pallas kernels  239 us (89%)
  local copies, waits for them, and re-layouts  16.7 us (6%)
  other arithmetic  5.74 us (2%)
  matrix products  4.46 us (2%)
  between operations  4 us (1%)
    pallas_call x1, Pallas kernels, main_call(): pl.pallas_call(functools.partial(main_kernel, block), in_specs=[pl.BlockS...  161 us
    pallas_call x1, Pallas kernels, sum_call(): pl.pallas_call(sum_kernel, in_specs=[vmem] * 5, out_specs=[hbm, hbm, vmem...  77.9 us
    unnamed x44, local copies, waits for them, and re-layouts  16.1 us

profile of v3, /device:TPU:1, one launch (start us, length us, event | category | flops | bytes accessed | tf_op | source)
XLA Modules:
  0.0 269.4 jit_solution(10790441766445257642)
XLA Ops:
  2.0 0.6 pad_maximum_fusion.1.scal
  2.6 3.9 %multiply_reduce_fusion.3 = (f32[256]{0:T(256)S(1)}, f32[256,1024]{1,0:T(8,128)S(1)}) fusion(bf16[256,2048]{1,0:T(8,128)(2,1)} %img_x.3, bf16[2048,1024]{1,0:T(8,128)(2,1)} %param.8), kind=kOutput, calls=%fused_computation.10 | convolution fusion | flops 1074265856 | bytes 6292480 | tf_op jit(solution)/shard_map/dot_general | solution.py:22
  6.5 0.6 copy-done.13
  7.2 0.9 multiply_convert_fusion.1.img_own
  8.1 0.5 multiply_reduce_fusion.2
  8.6 0.6 copy-done.17
  9.2 0.4 copy-done.6
  9.6 0.6 copy-done.15
  10.2 0.9 multiply_convert_fusion.txt_own
  11.1 160.6 %scores.1 = (f32[256,1024]{1,0:T(8,128)}, f32[256,1024]{1,0:T(8,128)}, f32[3,8,128]{2,1,0:T(8,128)}, bf16[256,1280]{1,0:T(8,128)(2,1)}) custom-call(f32[2]{0:T(128)} %pad_maximum_fusion.1.scal, bf16[256,1024]{1,0:T(8,128)(2,1)} %multiply_convert_fusion.1.img_own, bf16[256,1024]{1,0:T(8,128)(2,1)} %multiply_convert_fusion.txt_own, bf16[256,2048]{1,0:T(8,128)(2,1)} %img_x.3, ...), custom_call_target="tpu_custom_call" | custom-call | tf_op jit(solution)/shard_map/scores/pallas_call | solution.py:451
  171.7 2.6 multiply_reduce_fusion
  174.5 0.2 fusion.2
  174.8 0.1 copy-done.9
  174.8 0.3 copy-done.10
  175.1 0.2 fusion.3
  175.4 0.1 pad_maximum_fusion.du_own
  175.5 0.3 copy-done.1
  175.8 0.2 copy-done.4
  176.0 77.9 %weights.1 = (f32[2048,1024]{1,0:T(8,128)S(1)}, f32[512,1024]{1,0:T(8,128)S(1)}, f32[3,8,128]{2,1,0:T(8,128)S(1)}) custom-call(bf16[256,2048]{1,0:T(8,128)(2,1)S(1)} %copy-done.1, bf16[256,512]{1,0:T(8,128)(2,1)S(1)} %copy-done.3, bf16[256,1280]{1,0:T(8,128)(2,1)S(1)} %copy-done.4, bf16[2,256,1024]{2,1,0:T(8,128)(2,1)S(1)} %pad_maximum_fusion.du_own, ...), custom_call_target="tpu_custom_call" | custom-call | tf_op jit(solution)/shard_map/weights/pallas_call | solution.py:641
  254.0 3.2 %copy-done = f32[2048,1024]{1,0:T(8,128)} copy-done((f32[2048,1024]{1,0:T(8,128)}, f32[2048,1024]{1,0:T(8,128)S(1)}, u32[]{:S(2)}) %copy-start) | copy-done | bytes 8388632
  257.2 0.1 reduce_sum.57
  257.3 0.6 fusion.4
  258.5 8.4 %copy.15 = f32[2048,1024]{1,0:T(8,128)} copy(f32[2048,1024]{1,0:T(8,128)} %copy-done) | data formatting | bytes 16777216
  267.0 1.3 copy.16
  (38 shorter events, 0.2 us)
Async XLA Ops:
  2.6 5.5 %copy-start.2 = (bf16[256,512]{1,0:T(8,128)(2,1)S(1)}, bf16[256,512]{1,0:T(8,128)(2,1)}, u32[]{:S(2)}) copy-start(bf16[256,512]{1,0:T(8,128)(2,1)} %txt_x.3) | copy-start | bytes 786436
  2.6 5.5 %copy-start.12 = (bf16[512,1024]{1,0:T(8,128)(2,1)S(1)}, bf16[512,1024]{1,0:T(8,128)(2,1)}, u32[]{:S(2)}) copy-start(bf16[512,1024]{1,0:T(8,128)(2,1)} %param.9) | copy-start | bytes 3145732
  6.5 2.1 copy-start.8
  6.5 2.7 copy-start.19
  6.5 0.6 copy-start.13
  8.6 0.6 copy-start.17
  8.6 1.0 copy-start.6
  9.6 0.6 copy-start.15
  171.7 2.7 %copy-start.18 = (f32[256]{0:T(256)S(1)}, f32[256]{0:T(256)}, u32[]{:S(2)}) copy-start(f32[256]{0:T(256)} %copy-done.17) | copy-start | bytes 3076
  171.7 2.8 %copy-start.7 = (f32[256,1024]{1,0:T(8,128)S(1)}, f32[256,1024]{1,0:T(8,128)}, u32[]{:S(2)}) copy-start(f32[256,1024]{1,0:T(8,128)} %copy-done.6) | copy-start | bytes 3145732
  171.7 2.8 %copy-start.11 = (f32[256,1024]{1,0:T(8,128)S(1)}, f32[256,1024]{1,0:T(8,128)}, u32[]{:S(2)}) copy-start(f32[256,1024]{1,0:T(8,128)} %get-tuple-element.14) | copy-start | bytes 3145732
  171.7 2.8 %copy-start.16 = (f32[256]{0:T(256)S(1)}, f32[256]{0:T(256)}, u32[]{:S(2)}) copy-start(f32[256]{0:T(256)} %copy-done.15) | copy-start | bytes 3076
  171.7 3.0 %copy-start.20 = (f32[256]{0:T(256)S(1)}, f32[256]{0:T(256)}, u32[]{:S(2)}) copy-start(f32[256]{0:T(256)} %copy-done.19) | copy-start | bytes 3076
  171.7 3.1 %copy-start.9 = (f32[256,1024]{1,0:T(8,128)S(1)}, f32[256,1024]{1,0:T(8,128)}, u32[]{:S(2)}) copy-start(f32[256,1024]{1,0:T(8,128)} %copy-done.8) | copy-start | bytes 3145732
  171.7 3.4 %copy-start.10 = (f32[256,1024]{1,0:T(8,128)S(1)}, f32[256,1024]{1,0:T(8,128)}, u32[]{:S(2)}) copy-start(f32[256,1024]{1,0:T(8,128)} %get-tuple-element.13) | copy-start | bytes 3145732
  171.7 3.4 %copy-start.14 = (f32[256]{0:T(256)S(1)}, f32[256]{0:T(256)}, u32[]{:S(2)}) copy-start(f32[256]{0:T(256)} %copy-done.13) | copy-start | bytes 3076
  174.4 1.4 copy-start.1
  174.4 1.4 copy-start.3
  174.4 1.6 copy-start.4
  174.4 1.6 copy-start.5
  254.0 3.2 %copy-start = (f32[2048,1024]{1,0:T(8,128)}, f32[2048,1024]{1,0:T(8,128)S(1)}, u32[]{:S(2)}) copy-start(f32[2048,1024]{1,0:T(8,128)S(1)} %get-tuple-element.36) | copy-start | bytes 25165828

commit v4 on v3

--- a/solution.py
+++ b/solution.py
@@ -14,14 +14,9 @@
 VMEM_LIMIT = 67043328
 
 
-def normalize(raw):
-    return raw * lax.rsqrt(jnp.sum(raw * raw, axis=-1, keepdims=True))
-
-
 def embed_rows(feat_x, w_proj):
-    raw_emb = jnp.dot(feat_x, w_proj, preferred_element_type=F32)
-    unit_emb, pull_back = jax.vjp(normalize, raw_emb)
-    return unit_emb.astype(BF16), pull_back
+    raw = jnp.dot(feat_x, w_proj, preferred_element_type=F32)
+    return raw, (raw * lax.rsqrt(jnp.sum(raw * raw, axis=-1, keepdims=True))).astype(BF16)
 
 
 class Place:
@@ -77,10 +72,11 @@
 
 
 class Wire:
-    def __init__(self, send, recv):
-        self.send, self.recv, self.open = send, recv, []
+    def __init__(self, send, recv, first=0):
+        self.send, self.recv, self.first, self.open = send, recv, first, []
 
     def copy(self, k, src, dst, dev):
+        k += self.first
         return pltpu.make_async_remote_copy(src_ref=src, dst_ref=dst, send_sem=self.send.at[k], recv_sem=self.recv.at[k], device_id=dev, device_id_type=MESH)
 
     def go(self, *what):
@@ -97,8 +93,8 @@
 
 
 class Pieces:
-    def __init__(self, send, recv):
-        self.wire = Wire(send, recv)
+    def __init__(self, *where):
+        self.wire = Wire(*where)
 
     def go(self, k, src, dst, dev):
         for p in range(2):
@@ -114,6 +110,8 @@
 
 GATHER_COPIES = 8
 SCATTER_COPIES = 10
+OWN, RIGHT, LEFT, FAR = ((0, step) for step in (0, 1, -1, 2))
+TWIN, TWIN_RIGHT, TWIN_LEFT, TWIN_FAR = ((1, step) for step in (0, 1, -1, 2))
 
 
 def gather_stages(wire, g, own, blk, half, relative, seen=None):
@@ -123,7 +121,8 @@
         twin, step = key
         if not relative:
             return key
-        return {"right": (twin, step - 1), "left": (twin, step + 1), "pair": (not twin, step)}[way]
+        twin, step = {"right": (twin, step - 1), "left": (twin, step + 1), "pair": (1 - twin, step)}[way]
+        return twin, (step + 1) % 4 - 1
 
     def send(k, key, way, h=None):
         dev = getattr(g, way)
@@ -132,40 +131,40 @@
 
     def start():
         for k, way in enumerate(("right", "left", "pair")):
-            wire.go(k, own, blk(moved((False, 0), way)), getattr(g, way))
+            wire.go(k, own, blk(moved(OWN, way)), getattr(g, way))
 
     def ring():
-        wire.got(0, blk((False, -1)), g.left)
-        send(3, (False, -1), "right", 0)
-        wire.got(1, blk((False, 1)), g.right)
-        send(4, (False, 1), "left", 1)
-        seen((False, -1))
-        seen((False, 1))
+        wire.got(0, blk(LEFT), g.left)
+        send(3, LEFT, "right", 0)
+        wire.got(1, blk(RIGHT), g.right)
+        send(4, RIGHT, "left", 1)
+        seen(LEFT)
+        seen(RIGHT)
 
     def twin():
-        wire.got(2, blk((True, 0)), g.pair)
-        send(5, (True, 0), "right")
-        send(6, (True, 0), "left")
-        seen((True, 0))
+        wire.got(2, blk(TWIN), g.pair)
+        send(5, TWIN, "right")
+        send(6, TWIN, "left")
+        seen(TWIN)
 
     def across():
-        wire.got(3, half((False, 2), 0), g.left)
-        wire.got(4, half((False, 2), 1), g.right)
-        send(7, (False, 2), "pair")
-        seen((False, 2))
+        wire.got(3, half(FAR, 0), g.left)
+        wire.got(4, half(FAR, 1), g.right)
+        send(7, FAR, "pair")
+        seen(FAR)
 
     def last():
-        wire.got(5, blk((True, -1)), g.left)
-        wire.got(6, blk((True, 1)), g.right)
-        seen((True, -1))
-        seen((True, 1))
-        wire.got(7, blk((True, 2)), g.pair)
-        seen((True, 2))
+        wire.got(5, blk(TWIN_LEFT), g.left)
+        wire.got(6, blk(TWIN_RIGHT), g.right)
+        seen(TWIN_LEFT)
+        seen(TWIN_RIGHT)
+        wire.got(7, blk(TWIN_FAR), g.pair)
+        seen(TWIN_FAR)
 
     return [start, ring, twin, across, last]
 
 
-SEEN = [(False, 0), (False, -1), (False, 1), (True, 0), (False, 2), (True, -1), (True, 1), (True, 2)]
+SEEN = [OWN, LEFT, RIGHT, TWIN, FAR, TWIN_LEFT, TWIN_RIGHT, TWIN_FAR]
 
 
 class Scatter:
@@ -173,43 +172,43 @@
         self.wire, self.g, self.blk, self.half, self.finish = wire, g, blk, half, finish
         whole, part = bufs
         self.rp, self.rr0, self.rr1, self.rf0, self.rf1, self.rf2 = (whole.at[k] for k in range(6))
-        self.rh0, self.rh1 = part.at[0], part.at[1]
-        rows = part.shape[1]
-        self.lo, self.hi = pl.ds(0, rows), pl.ds(rows, rows)
+        rows, cut = whole.shape[1], part.shape[1]
+        self.lo, self.hi = pl.ds(0, cut), pl.ds(cut, rows - cut)
+        self.rh0, self.rh1 = part.at[0], part.at[1, pl.ds(0, rows - cut)]
 
     def twins(self):
-        self.wire.go(1, self.blk((True, 1)), self.rr0, self.g.right)
-        self.wire.go(2, self.blk((True, -1)), self.rr1, self.g.left)
+        self.wire.go(1, self.blk(TWIN_RIGHT), self.rr0, self.g.right)
+        self.wire.go(2, self.blk(TWIN_LEFT), self.rr1, self.g.left)
 
     def opposite(self):
-        self.wire.go(0, self.blk((True, 2)), self.rp, self.g.pair)
+        self.wire.go(0, self.blk(TWIN_FAR), self.rp, self.g.pair)
 
     def early(self):
-        self.wire.go(3, self.half((False, 1), 1), self.rf0.at[self.hi], self.g.right)
-        self.wire.go(4, self.half((False, -1), 0), self.rf1.at[self.lo], self.g.left)
+        self.wire.go(3, self.half(RIGHT, 1), self.rf0.at[self.hi], self.g.right)
+        self.wire.go(4, self.half(LEFT, 0), self.rf1.at[self.lo], self.g.left)
 
     def across(self):
         self.wire.got(0, self.rp, self.g.pair)
         for h, sl in ((0, self.lo), (1, self.hi)):
-            v = self.half((False, 2), h)
+            v = self.half(FAR, h)
             v[...] += self.rp[sl]
-        self.wire.go(5, self.half((False, 2), 0), self.rh0, self.g.right)
-        self.wire.go(6, self.half((False, 2), 1), self.rh1, self.g.left)
+        self.wire.go(5, self.half(FAR, 0), self.rh0, self.g.right)
+        self.wire.go(6, self.half(FAR, 1), self.rh1, self.g.left)
 
     def twin(self):
         self.wire.got(1, self.rr0, self.g.left)
         self.wire.got(2, self.rr1, self.g.right)
-        v = self.blk((True, 0))
+        v = self.blk(TWIN)
         v[...] += self.rr0[...] + self.rr1[...]
         self.wire.go(7, v, self.rf2, self.g.pair)
 
     def ring(self):
         self.wire.got(5, self.rh0, self.g.left)
-        v = self.half((False, 1), 0)
+        v = self.half(RIGHT, 0)
         v[...] += self.rh0[...]
         self.wire.go(8, v, self.rf0.at[self.lo], self.g.right)
         self.wire.got(6, self.rh1, self.g.right)
-        v = self.half((False, -1), 1)
+        v = self.half(LEFT, 1)
         v[...] += self.rh1[...]
         self.wire.go(9, v, self.rf1.at[self.hi], self.g.left)
 
@@ -236,12 +235,12 @@
         fb()
 
 
-PLACE = {(False, 0): 0, (True, 0): 1, (False, 1): 2, (False, 3): 3, (True, 2): 4, (False, 2): 5, (True, 1): 6, (True, 3): 7}
+PLACE = {key: k for k, key in enumerate((OWN, TWIN, RIGHT, LEFT, TWIN_FAR, FAR, TWIN_RIGHT, TWIN_LEFT))}
 
 
 def rows_of(ref, size, base=0):
     def at(key):
-        return base + PLACE[key[0], key[1] % 4] * size
+        return base + PLACE[key] * size
 
     def blk(key):
         return ref.at[pl.ds(at(key), size)]
@@ -296,8 +295,8 @@
     other_blk, _ = rows_of(txt, block)
     wi, wt, core = Wire(ig_s, ig_r), Wire(tg_s, tg_r), Wire(core_s, core_r)
 
-    own_i = pltpu.make_async_copy(img_own, img_blk((False, 0)), local.at[0])
-    own_t = pltpu.make_async_copy(txt_own, txt_blk((False, 0)), local.at[1])
+    own_i = pltpu.make_async_copy(img_own, img_blk(OWN), local.at[0])
+    own_t = pltpu.make_async_copy(txt_own, txt_blk(OWN), local.at[1])
     own_i.start()
     own_t.start()
     own_i.wait()
@@ -307,11 +306,11 @@
     def share(key):
         core.go(next(sent), txt_blk(key), other_blk(key), partner)
 
-    a = gather_stages(wi, gi, img_blk((False, 0)), img_blk, img_half, True)
-    b = gather_stages(wt, gt, txt_blk((False, 0)), txt_blk, txt_half, True, share)
+    a = gather_stages(wi, gi, img_blk(OWN), img_blk, img_half, True)
+    b = gather_stages(wt, gt, txt_blk(OWN), txt_blk, txt_half, True, share)
     a[0]()
     b[0]()
-    share((False, 0))
+    share(OWN)
     img_f, txt_f = img_x.shape[1] // 2, txt_x.shape[1] // 2
     core.go(8, img_x.at[:, pl.ds(pl.multiple_of((1 - c) * img_f, img_f), img_f)], x_got.at[:, pl.ds(0, img_f)], partner)
     core.go(9, txt_x.at[:, pl.ds(pl.multiple_of((1 - c) * txt_f, txt_f), txt_f)], x_got.at[:, pl.ds(img_f, txt_f)], partner)
@@ -341,8 +340,8 @@
         return done
 
     wi, wt = Wire(is_s, is_r), Wire(ts_s, ts_r)
-    ri = Scatter(wi, gi, di_blk, di_half, (ibuf, ihalf), finish(d_img_out, di_blk((False, 0)), 0))
-    rt = Scatter(wt, gt, dt_blk, dt_half, (tbuf, thalf), finish(d_txt_out, dt_blk((False, 0)), 1))
+    ri = Scatter(wi, gi, di_blk, di_half, (ibuf, ihalf), finish(d_img_out, di_blk(OWN), 0))
+    rt = Scatter(wt, gt, dt_blk, dt_half, (tbuf, thalf), finish(d_txt_out, dt_blk(OWN), 1))
 
     def hand(k):
         return pltpu.make_async_remote_copy(
@@ -480,123 +479,148 @@
     )(scal, img_emb, txt_emb, img_x, txt_x)
 
 
+def pull_back(raw, cot):
+    inv = lax.rsqrt(jnp.sum(raw * raw, axis=-1, keepdims=True))
+    along = jnp.sum(cot * raw, axis=-1, keepdims=True) * (inv * inv)
+    return (inv * (cot - raw * along)).astype(BF16)
+
+
+COLOURS = 4
+
+
 def sum_kernel(
-    img_x, txt_x, x_got, du_own, sums_in, d_w_img, d_w_txt, sums,
-    w, w2, du, abuf, ahalf, bbuf, bhalf, abuf2, ahalf2, bbuf2, bhalf2, small,
-    du_s, du_r, a1s, a1r, b1s, b1r, a2s, a2r, b2s, b2r, a3s, a3r, b3s, b3r, a4s, a4r, b4s, b4r, d_s, d_r, q_s, q_r, local,
+    scal, img_x, txt_x, x_got, img_raw, txt_raw, d_img, d_txt, sums_in, d_w_img, d_w_txt, sums,
+    w, w2, du_own, du, buf1, half1, buf2, half2, small,
+    du_s, du_r, sc_s, sc_r, ga_s, ga_r, out_s, out_r, core_s, core_r, small_s, small_r, local,
 ):
     place = Place()
-    gi, gt = place.image_group(), place.text_group()
-    c = place.c
-    partner = place.partner()
+    c, partner = place.c, place.partner()
+    du_own[0] = pull_back(img_raw[...], scal[2] * d_img[...])
+    du_own[1] = pull_back(txt_raw[...], scal[2] * d_txt[...])
     greet(place)
+    pre = Wire(du_s, du_r)
+    pre.go(0, du_own, du, partner)
     img_f, txt_f = img_x.shape[1] // 2, txt_x.shape[1] // 2
     ni, nt = img_f // 16, txt_f // 16
-    rows, lanes = ni + nt, w.shape[1] // 8
-    pre = Wire(du_s, du_r)
-    pre.go(0, du_own, du, partner)
+    rows, wide = ni + nt, w.shape[1] // 2
+    tall, lanes, cut = rows // 2, wide // 4, half2.shape[2]
 
     def outer(lhs, rhs):
         return lax.dot_general(lhs, rhs, (((0,), (0,)), ((), ())), preferred_element_type=F32)
 
-    def weights(own, part):
-        rhs = du_own if own else du
-        for k in range(img_f // 128):
-            cols = pl.ds(pl.multiple_of(c * img_f + k * 128, 128), 128)
-            lhs = img_x[:, cols] if own else x_got[:, k * 128 : (k + 1) * 128]
-            put(part, k * 128, 128, ni, 0, outer(lhs, rhs[0]), own)
-        for k in range(txt_f // 128):
-            cols = pl.ds(pl.multiple_of(c * txt_f + k * 128, 128), 128)
-            lhs = txt_x[:, cols] if own else x_got[:, img_f + k * 128 : img_f + (k + 1) * 128]
-            put(part, k * 128, 128, nt, ni, outer(lhs, rhs[1]), own)
-
-    def put(ref, first, count, size, shift, val, fresh):
-        for b in range(count // size):
-            at = ((first + b * size) // size) * rows + shift
+    def put(first, size, shift, val, fresh):
+        for b in range(val.shape[0] // size):
+            at = (first // size + b) * rows + shift
             piece = val[b * size : (b + 1) * size]
             if fresh:
-                ref[at : at + size] = piece
+                w[at : at + size] = piece
             else:
-                ref[at : at + size] += piece
-
-    weights(True, w)
+                w[at : at + size] += piece
+
+    def weights(own):
+        rhs = du_own if own else du
+        lane = 128
+        for k in range(0, img_f, lane):
+            cols = pl.ds(pl.multiple_of(c * img_f + k, lane), lane)
+            put(k, ni, 0, outer(img_x[:, cols] if own else x_got[:, k : k + lane], rhs[0]), own)
+        for k in range(0, txt_f, lane):
+            cols = pl.ds(pl.multiple_of(c * txt_f + k, lane), lane)
+            put(k, nt, ni, outer(txt_x[:, cols] if own else x_got[:, img_f + k : img_f + k + lane], rhs[1]), own)
+
+    weights(True)
     pre.got(0, du, partner)
-    weights(False, w)
+    weights(False)
     pre.drain()
 
-    small_wire = Wire(q_s, q_r)
-    hops = [
-        place.at(x=place.near(place.x)), place.at(x=place.far(place.x)), place.at(y=place.near(place.y)), place.at(y=place.far(place.y)),
-        place.at(z=place.near(place.z)), place.at(z=place.far(place.z)), partner,
-    ]
+    small_wire = Wire(small_s, small_r)
+    hops = []
+    for name in "xyz":
+        v = getattr(place, name)
+        hops += [place.at(**{name: place.near(v)}), place.at(**{name: place.far(v)})]
+    hops.append(partner)
     small[0] = sums_in[...]
 
-    def small_send(k):
-        small_wire.go(k, small.at[2 * k], small.at[2 * k + 1], hops[k])
-
-    def small_take(k):
-        small_wire.got(k, small.at[2 * k + 1], hops[k])
-        small[2 * k + 2] = small[2 * k] + small[2 * k + 1]
-
-    dwire = Pieces(d_s, d_r)
+    def small_step(n):
+        if 0 < n <= len(hops):
+            k = n - 1
+            small_wire.got(k, small.at[2 * k + 1], hops[k])
+            small[2 * n] = small[2 * k] + small[2 * k + 1]
+        if n < len(hops):
+            small_wire.go(n, small.at[2 * n], small.at[2 * n + 1], hops[n])
+
+    dwire = Pieces(core_s, core_r)
     copies = []
 
-    def colour(n, g1, g2, s1, s2, s3, s4, buf1, half1, buf2, half2):
-        base = n * 8 * rows
-        mine = base + g1.slot((False, 0)) * rows
-
-        def sl(first, count):
-            return pl.ds(pl.multiple_of(first, count), count)
+    def sl(first, count):
+        return pl.ds(pl.multiple_of(first, count), count)
+
+    def rows_at(first, count):
+        return pl.ds(pl.multiple_of(first, 8), count)
+
+    def colour(n):
+        order = (place.image_group(), place.text_group())
+        g1, g2 = order if n % 2 == 0 else order[::-1]
+        group = n % 2 * 8
+        base = group * rows
+        across = pl.ds(n // 2 * wide, wide)
+        mine = base + g1.slot(OWN) * rows
+        keep = n % 2 * rows
 
         def w_blk(key):
-            return w.at[sl(base + g1.slot(key) * rows, rows)]
+            return w.at[sl(base + g1.slot(key) * rows, rows), across]
 
         def w_half(key, h):
-            return w.at[sl(base + g1.slot(key) * rows + h * (rows // 2), rows // 2)]
+            return w.at[sl(base + g1.slot(key) * rows + h * tall, tall), across]
 
         def strip(ref, first):
+            def at(key):
+                slot = g2.slot(key)
+                return first + lax.div(slot, 4) * tall, sl(n // 2 * wide + lax.rem(slot, 4) * lanes, lanes)
+
             def blk(key):
-                return ref.at[sl(first, rows), sl(g2.slot(key) * lanes, lanes)]
+                top, cols = at(key)
+                return ref.at[rows_at(top, tall), cols]
 
             def half(key, h):
-                return ref.at[sl(first + h * (rows // 2), rows // 2), sl(g2.slot(key) * lanes, lanes)]
+                top, cols = at(key)
+                return ref.at[rows_at(top + h * cut, tall - cut if h else cut), cols]
 
             return blk, half
 
+        def outs(key, core, h, parts):
+            at = group + g1.slot(key)
+            a, b = ni // parts, nt // parts
+            return (
+                d_w_img.at[sl(core * img_f + at * ni + h * a, a), across],
+                d_w_txt.at[sl(core * txt_f + at * nt + h * b, b), across],
+            )
+
+        def o_blk(key, core=c):
+            return outs(key, core, 0, 1)
+
         def o_half(key, h):
-            i0 = c * img_f + (n * 8 + g1.slot(key)) * ni
-            t0 = c * txt_f + (n * 8 + g1.slot(key)) * nt
-            return d_w_img.at[sl(i0 + h * (ni // 2), ni // 2)], d_w_txt.at[sl(t0 + h * (nt // 2), nt // 2)]
-
-        def o_blk(key, core=c):
-            i0 = core * img_f + (n * 8 + g1.slot(key)) * ni
-            t0 = core * txt_f + (n * 8 + g1.slot(key)) * nt
-            return d_w_img.at[sl(i0, ni)], d_w_txt.at[sl(t0, nt)]
-
-        w1, wire2, w3 = Wire(*s1), Wire(*s2), Wire(*s3)
-        w4 = Pieces(*s4)
+            return outs(key, c, h, 2)
+
         ws_blk, ws_half = strip(w, mine)
-        os_blk, os_half = strip(w2, n * rows)
-        home = (False, 0)
+        os_blk, os_half = strip(w2, keep)
 
         def done1(p, q, r):
-            v = w_blk(home)
+            v = w_blk(OWN)
             v[...] += p[...] + q[...] + r[...]
 
         def done2(p, q, r):
-            v = os_blk(home)
-            v[...] = ws_blk(home)[...] + p[...] + q[...] + r[...]
-
-        count = [n * 8]
-        whole = w2.at[n * rows : n * rows + ni], w2.at[n * rows + ni : (n + 1) * rows]
+            v = os_blk(OWN)
+            v[...] = ws_blk(OWN)[...] + p[...] + q[...] + r[...]
+
+        whole = w2.at[pl.ds(keep, ni), across], w2.at[pl.ds(keep + ni, nt), across]
+        turn = iter(range(n * 8, n * 8 + 8))
 
         def share(key, src=None):
-            dwire.go(count[0], o_blk(key) if src is None else src, o_blk(key), partner)
-            count[0] += 1
+            dwire.go(next(turn), o_blk(key) if src is None else src, o_blk(key), partner)
 
         def share_own():
-            share(home, whole)
-            for p, (src, dst) in enumerate(zip(whole, o_blk(home))):
+            share(OWN, whole)
+            for p, (src, dst) in enumerate(zip(whole, o_blk(OWN))):
                 copy = pltpu.make_async_copy(src, dst, local.at[2 * n + p])
                 copy.start()
                 copies.append(copy)
@@ -605,42 +629,44 @@
             for k, key in enumerate(SEEN):
                 dwire.got(n * 8 + k, o_blk(key, 1 - c), partner)
 
-        stages = Scatter(w1, g1, w_blk, w_half, (buf1, half1), done1).stages()
-        stages += Scatter(wire2, g2, ws_blk, ws_half, (buf2, half2), done2).stages()
-        stages += gather_stages(w3, g2, os_blk(home), os_blk, os_half, False)
+        w1, w2_, w3 = (Wire(*args) for args in ((sc_s, sc_r, n * SCATTER_COPIES), (sc_s, sc_r, (COLOURS + n) * SCATTER_COPIES), (ga_s, ga_r, n * GATHER_COPIES)))
+        w4 = Pieces(out_s, out_r, 2 * n * GATHER_COPIES)
+        stages = Scatter(w1, g1, w_blk, w_half, (buf1.at[n], half1.at[n]), done1).stages()
+        stages += Scatter(w2_, g2, ws_blk, ws_half, (buf2.at[n], half2.at[n]), done2).stages()
+        stages += gather_stages(w3, g2, os_blk(OWN), os_blk, os_half, False)
         tail = gather_stages(w4, g1, whole, o_blk, o_half, False, share)
         stages += [tail[0], share_own] + tail[1:] + [got_shares]
-        return stages, [w1, wire2, w3, w4]
-
-    sa, wa = colour(0, gi, gt, (a1s, a1r), (a2s, a2r), (a3s, a3r), (a4s, a4r), abuf, ahalf, abuf2, ahalf2)
-    sb, wb = colour(1, gt, gi, (b1s, b1r), (b2s, b2r), (b3s, b3r), (b4s, b4r), bbuf, bhalf, bbuf2, bhalf2)
-    for n, (fa, fb) in enumerate(zip(sa, sb)):
-        fa()
-        fb()
-        if 0 < n < 8:
-            small_take(n - 1)
-        if n < 7:
-            small_send(n)
-    sums[...] = small[14]
+        return stages, [w1, w2_, w3, w4]
+
+    colours = [colour(n) for n in range(COLOURS)]
+    for n in range(len(colours[0][0]) + 1):
+        for k, (stages, _) in enumerate(colours):
+            at = n - k // 2
+            if 0 <= at < len(stages):
+                stages[at]()
+        small_step(n)
+    sums[...] = small[2 * len(hops)]
     for copy in copies:
         copy.wait()
-    for wire in wa + wb + [dwire, small_wire]:
-        wire.drain()
-
-
-def sum_call(img_x, txt_x, x_got, du, sums):
-    block = img_x.shape[0]
-    feats = x_got.shape[1]
-    dim = du.shape[2]
+    for _, wires in colours:
+        for wire in wires:
+            wire.drain()
+    dwire.drain()
+    small_wire.drain()
+
+
+def sum_call(scal, img_x, txt_x, x_got, img_raw, txt_raw, d_img, d_txt, sums):
+    block, feats = x_got.shape
+    dim = d_img.shape[1]
     vmem = pl.BlockSpec(memory_space=pltpu.VMEM)
     hbm = pl.BlockSpec(memory_space=pl.ANY)
-    sem = pltpu.SemaphoreType.DMA
+    sem = lambda n: [pltpu.SemaphoreType.DMA((n,))] * 2
     f = lambda *s: pltpu.VMEM(s, F32)
-    rows, lanes = feats // 16, dim // 8
-    sc, ga, ga2 = sem((SCATTER_COPIES,)), sem((GATHER_COPIES,)), sem((2 * GATHER_COPIES,))
+    rows, wide = feats // 16, dim // 2
+    tall, lanes, cut = rows // 2, wide // 4, 24
     return pl.pallas_call(
         sum_kernel,
-        in_specs=[vmem] * 5,
+        in_specs=[pl.BlockSpec(memory_space=pltpu.SMEM)] + [vmem] * 8,
         out_specs=[hbm, hbm, vmem],
         out_shape=[
             jax.ShapeDtypeStruct((img_x.shape[1], dim), F32),
@@ -650,18 +676,43 @@
         scratch_shapes=[
             f(feats, dim),
             f(2 * rows, dim),
-            pltpu.VMEM(du.shape, BF16),
-            f(6, rows, dim), f(2, rows // 2, dim), f(6, rows, dim), f(2, rows // 2, dim),
-            f(6, rows, lanes), f(2, rows // 2, lanes), f(6, rows, lanes), f(2, rows // 2, lanes),
+            pltpu.VMEM((2, block, dim), BF16),
+            pltpu.VMEM((2, block, dim), BF16),
+            f(COLOURS, 6, rows, wide), f(COLOURS, 2, tall, wide),
+            f(COLOURS, 6, tall, lanes), f(COLOURS, 2, cut, lanes),
             f(15, *sums.shape),
-            sem((1,)), sem((1,)),
-            sc, sc, sc, sc, sc, sc, sc, sc,
-            ga, ga, ga, ga, ga2, ga2, ga2, ga2,
-            sem((32,)), sem((32,)), sem((7,)), sem((7,)), sem((4,)),
+            *sem(1), *sem(2 * COLOURS * SCATTER_COPIES), *sem(COLOURS * GATHER_COPIES), *sem(2 * COLOURS * GATHER_COPIES),
+            *sem(2 * COLOURS * 8), *sem(7), pltpu.SemaphoreType.DMA((2 * COLOURS,)),
         ],
-        compiler_params=pltpu.CompilerParams(collective_id=1, has_side_effects=True, vmem_limit_bytes=28 * 2**20),
+        compiler_params=pltpu.CompilerParams(collective_id=1, has_side_effects=True, vmem_limit_bytes=32 * 2**20),
         name="weights",
-    )(img_x, txt_x, x_got, du, sums)
+    )(scal, img_x, txt_x, x_got, img_raw, txt_raw, d_img, d_txt, sums)
+
+
+def store_kernel(total_rows, scal, sums, src_a, src_b, loss, d_temp, d_bias, dst_a, dst_b, sems):
+    copies = [pltpu.make_async_copy(src_a, dst_a, sems.at[0]), pltpu.make_async_copy(src_b, dst_b, sems.at[1])]
+    for copy in copies:
+        copy.start()
+    loss[0] = jnp.sum(sums[0]) / total_rows
+    d_temp[0] = scal[0] * (jnp.sum(sums[1]) / total_rows)
+    d_bias[0] = jnp.sum(sums[2]) / total_rows
+    for copy in copies:
+        copy.wait()
+
+
+def store_call(total_rows, scal, sums, *arrays):
+    hbm = pl.BlockSpec(memory_space=pl.ANY)
+    smem = pl.BlockSpec(memory_space=pltpu.SMEM)
+    one = jax.ShapeDtypeStruct((1,), F32)
+    return pl.pallas_call(
+        functools.partial(store_kernel, total_rows),
+        in_specs=[smem, pl.BlockSpec(memory_space=pltpu.VMEM), hbm, hbm],
+        out_specs=[smem] * 3 + [pl.BlockSpec(memory_space=pltpu.HBM)] * 2,
+        out_shape=[one] * 3 + [jax.ShapeDtypeStruct(a.shape, a.dtype) for a in arrays],
+        scratch_shapes=[pltpu.SemaphoreType.DMA((2,))],
+        compiler_params=pltpu.CompilerParams(vmem_limit_bytes=2**20),
+        name="store",
+    )(scal, sums, *arrays)
 
 
 def solution(mesh):
@@ -671,17 +722,13 @@
     def local_fn(img_x, txt_x, w_img, w_txt, log_temp, logit_bias):
         block = img_x.shape[0]
         total_rows = block * dev_count
-        txt_emb, txt_pull = embed_rows(txt_x, w_txt)
-        img_emb, img_pull = embed_rows(img_x, w_img)
+        txt_raw, txt_emb = embed_rows(txt_x, w_txt)
+        img_raw, img_emb = embed_rows(img_x, w_img)
         temp_scale = jnp.exp(log_temp[0])
-        scal = jnp.stack([temp_scale, logit_bias[0]])
+        scal = jnp.stack([temp_scale, logit_bias[0], temp_scale / total_rows])
         d_img, d_txt, sums, x_got = main_call(scal, img_emb, txt_emb, img_x, txt_x)
-        post = temp_scale / total_rows
-        d_img_raw = img_pull(post * d_img)[0].astype(BF16)
-        d_txt_raw = txt_pull(post * d_txt)[0].astype(BF16)
-        d_w_img, d_w_txt, sums = sum_call(img_x, txt_x, x_got, jnp.stack([d_img_raw, d_txt_raw]), sums)
-        parts = jnp.sum(sums, axis=(1, 2)) / total_rows
-        return parts[0:1], temp_scale * parts[1:2], parts[2:3], d_w_img, d_w_txt
+        d_w_img, d_w_txt, sums = sum_call(scal, img_x, txt_x, x_got, img_raw, txt_raw, d_img, d_txt, sums)
+        return tuple(store_call(total_rows, scal, sums, d_w_img, d_w_txt))
 
     batch_spec = P(batch_axes, None)
     return jax.shard_map(local_fn, mesh=mesh, in_specs=(batch_spec, batch_spec, P(), P(), P(), P()), out_specs=(P(), P(), P(), P(), P()), check_vma=False)

time: 270 us -> 265 us (0.981)
  local copies, waits for them, and re-layouts: 16.7 us -> 10.5 us
  Pallas kernels: 239 us -> 245 us
  other arithmetic: 5.74 us -> 1.75 us
    pallas_call x1 -> x2, Pallas kernels: 77.9 us -> 84.5 us  [the longest x1 79.4 us: sum_call(): pl.pallas_call(sum_kernel, in_specs=[pl.BlockSpec(memory_space=pltpu.SMEM...]
    unnamed x44 -> x26, local copies, waits for them, and re-layouts: 16.1 us -> 10.5 us
    reduce_sum x2 -> x0, other arithmetic: 2.71 us -> none  [the longest x1 2.6 us: normalize(): return raw * lax.rsqrt(jnp.sum(raw * raw, axis=-1, keepdims=True))]
where the time goes in v4:
time: 265 us; the launch traced here: 264 us
  Pallas kernels  245 us (92%)
  local copies, waits for them, and re-layouts  10.5 us (4%)
  matrix products  4.36 us (2%)
    pallas_call x1, Pallas kernels, main_call(): pl.pallas_call(functools.partial(main_kernel, block), in_specs=[pl.BlockS...  161 us
    pallas_call x1, Pallas kernels, sum_call(): pl.pallas_call(sum_kernel, in_specs=[pl.BlockSpec(memory_space=pltpu.SMEM...  79.4 us
    unnamed x26, local copies, waits for them, and re-layouts  10.5 us

profile of v4, /device:TPU:1, one launch (start us, length us, event | category | flops | bytes accessed | tf_op | source)
XLA Modules:
  0.0 264.4 jit_solution(15501926525948336573)
XLA Ops:
  0.6 0.0 copy-start.5
  0.6 0.0 copy-start.12
  2.1 0.6 pad_maximum_fusion.scal
  2.7 3.8 %multiply_reduce_fusion.1 = (f32[256]{0:T(256)S(1)}, f32[256,1024]{1,0:T(8,128)S(1)}) fusion(bf16[256,2048]{1,0:T(8,128)(2,1)} %img_x.3, bf16[2048,1024]{1,0:T(8,128)(2,1)} %param.8), kind=kOutput, calls=%fused_computation.3 | convolution fusion | flops 1074265856 | bytes 6292480 | tf_op jit(solution)/shard_map/dot_general | solution.py:18
  6.5 0.0 copy-start.3
  6.5 0.0 copy-done.5
  6.5 0.0 copy-done.12
  6.6 0.5 multiply_reduce_fusion
  7.1 1.2 multiply_convert_fusion
  8.3 0.0 copy-done.3
  8.3 1.0 copy-done
  9.2 160.9 %scores.1 = (f32[256,1024]{1,0:T(8,128)}, f32[256,1024]{1,0:T(8,128)}, f32[3,8,128]{2,1,0:T(8,128)}, bf16[256,1280]{1,0:T(8,128)(2,1)}) custom-call(f32[3]{0:T(128)} %pad_maximum_fusion.scal, bf16[256,1024]{1,0:T(8,128)(2,1)} %get-tuple-element.24.img_own, bf16[256,1024]{1,0:T(8,128)(2,1)} %get-tuple-element.23.txt_own, bf16[256,2048]{1,0:T(8,128)(2,1)} %img_x.3, ...), custom_call_target="tpu_custom_call" | custom-call | tf_op jit(solution)/shard_map/scores/pallas_call | solution.py:450
  170.1 0.0 copy-start.1
  170.1 1.2 copy-done.1
  171.4 1.2 copy-done.2
  172.6 1.2 copy-done.4
  173.8 0.9 copy-done.6
  174.8 1.2 copy-done.7
  176.0 1.2 copy-done.8
  177.2 1.1 copy-done.9
  178.3 0.7 copy-done.10
  179.0 0.7 copy-done.11
  179.7 79.4 %weights.1 = (f32[2048,1024]{1,0:T(8,128)S(1)}, f32[512,1024]{1,0:T(8,128)S(1)}, f32[3,8,128]{2,1,0:T(8,128)S(1)}) custom-call(f32[3]{0:T(128)S(1)} %copy-done.11, bf16[256,2048]{1,0:T(8,128)(2,1)S(1)} %copy-done.2, bf16[256,512]{1,0:T(8,128)(2,1)S(1)} %copy-done.6, bf16[256,1280]{1,0:T(8,128)(2,1)S(1)} %copy-done.9, f32[256,1024]{1,0:T(8,128)S(1)} %copy-done.4, ...), custom_call_target="tpu_custom_call" | custom-call | tf_op jit(solution)/shard_map/weights/pallas_call | solution.py:667
  259.0 5.2 %store.1 = (f32[1]{0:T(128)}, f32[1]{0:T(128)}, f32[1]{0:T(128)}, f32[2048,1024]{1,0:T(8,128)}, f32[512,1024]{1,0:T(8,128)}) custom-call(f32[3]{0:T(128)S(1)} %copy-done.11, f32[3,8,128]{2,1,0:T(8,128)S(1)} %get-tuple-element.16.sums, f32[2048,1024]{1,0:T(8,128)S(1)} %get-tuple-element.17.src_a, f32[512,1024]{1,0:T(8,128)S(1)} %get-tuple-element.18.src_b), custom_call_target="tpu_custom_call" | custom-call | tf_op jit(solution)/shard_map/store/pallas_call | solution.py:707
  (11 shorter events, 0.0 us)
Async XLA Ops:
  0.6 5.9 %copy-start.5 = (bf16[256,512]{1,0:T(8,128)(2,1)S(1)}, bf16[256,512]{1,0:T(8,128)(2,1)}, u32[]{:S(2)}) copy-start(bf16[256,512]{1,0:T(8,128)(2,1)} %txt_x.3) | copy-start | bytes 786436
  0.6 5.9 %copy-start.12 = (bf16[512,1024]{1,0:T(8,128)(2,1)S(1)}, bf16[512,1024]{1,0:T(8,128)(2,1)}, u32[]{:S(2)}) copy-start(bf16[512,1024]{1,0:T(8,128)(2,1)} %param.9) | copy-start | bytes 3145732
  6.5 1.7 copy-start.3
  8.3 1.0 copy-start
  170.1 1.2 copy-start.1
  171.4 1.2 copy-start.2
  172.6 1.2 copy-start.4
  173.8 0.9 copy-start.6
  174.8 1.2 copy-start.7
  176.0 1.2 copy-start.8
  177.2 1.1 copy-start.9
  178.3 0.7 copy-start.10
  179.0 0.7 copy-start.11

commit v5 on v4

--- a/solution.py
+++ b/solution.py
@@ -274,11 +274,11 @@
     q = 3 - least(div(m, 7), 1) - least(div(m, 12), 1) - div(m, 15)
     r = m - (16 - (q + 1) * (q + 1))
     down = least(div(r, q + 1), 1)
-    return q + down * (r - q - 1 - q), r + down * (q - r)
+    return r + down * (q - r), q + down * (r - q - 1 - q)
 
 
 def main_kernel(
-    block, scal, img_own, txt_own, img_x, txt_x, d_img_out, d_txt_out, sums, x_got,
+    block, scal, img_own, txt_own, img_x, txt_x, img_raw, txt_raw, sums, pack,
     img, txt, d_img, d_txt, give, taken, sbuf, gbuf,
     ibuf, ihalf, tbuf, thalf,
     ig_s, ig_r, tg_s, tg_r, is_s, is_r, ts_s, ts_r, core_s, core_r, hand_s, hand_r, local, free,
@@ -312,17 +312,20 @@
     b[0]()
     share(OWN)
     img_f, txt_f = img_x.shape[1] // 2, txt_x.shape[1] // 2
-    core.go(8, img_x.at[:, pl.ds(pl.multiple_of((1 - c) * img_f, img_f), img_f)], x_got.at[:, pl.ds(0, img_f)], partner)
-    core.go(9, txt_x.at[:, pl.ds(pl.multiple_of((1 - c) * txt_f, txt_f), txt_f)], x_got.at[:, pl.ds(img_f, txt_f)], partner)
+    feats = img_f + txt_f
+
+    def half_of(which, count):
+        return pl.ds(pl.multiple_of(which * count, count), count)
+
+    core.go(8, img_x.at[:, half_of(1 - c, img_f)], pack.at[:, pl.ds(feats, img_f)], partner)
+    core.go(9, txt_x.at[:, half_of(1 - c, txt_f)], pack.at[:, pl.ds(feats + img_f, txt_f)], partner)
     for ref in (d_img, d_txt, give, sums):
         ref[...] = jnp.zeros_like(ref)
     run_both(a[1:], b[1:])
     for k, key in enumerate(SEEN):
         core.got(k, other_blk(key), partner)
-    core.got(8, x_got.at[:, pl.ds(0, img_f)], partner)
-    core.got(9, x_got.at[:, pl.ds(img_f, txt_f)], partner)
-    for wire in (wi, wt, core):
-        wire.drain()
+    wi.drain()
+    wt.drain()
 
     scale, bias = scal[0], scal[1]
     di_blk, di_half = rows_of(d_img, block)
@@ -330,18 +333,34 @@
 
     outs = []
 
-    def finish(out, mine, k):
+    def put(src, first, count, k):
+        copy = pltpu.make_async_copy(src, pack.at[:, pl.ds(first, count)], local.at[4 + k])
+        copy.start()
+        outs.append(copy)
+
+    def du_view(which, k):
+        return pack.at[:, pl.ds(2 * feats + (2 * which + k) * img.shape[1], img.shape[1])]
+
+    def finish(mine, raw, k):
+        first = k * block
+        step = 64
+
         def done(p, q, r):
-            mine[...] += p[...] + (q[...] + r[...])
-            copy = pltpu.make_async_copy(mine, out, local.at[k])
-            copy.start()
-            outs.append(copy)
+            def rows_of_du(n, carry):
+                at = pl.ds(pl.multiple_of(n * step, step), step)
+                total = mine[at, :] + p[at, :] + (q[at, :] + r[at, :])
+                img[pl.ds(pl.multiple_of(first + n * step, step), step), :] = pull_back(raw[at, :], scal[2] * total)
+                return carry
+
+            lax.fori_loop(0, block // step, rows_of_du, 0)
+            core.go(10 + k, img.at[pl.ds(first, block)], du_view(1, k), partner)
+            put(img.at[pl.ds(first, block)], 2 * feats + k * img.shape[1], img.shape[1], k)
 
         return done
 
     wi, wt = Wire(is_s, is_r), Wire(ts_s, ts_r)
-    ri = Scatter(wi, gi, di_blk, di_half, (ibuf, ihalf), finish(d_img_out, di_blk(OWN), 0))
-    rt = Scatter(wt, gt, dt_blk, dt_half, (tbuf, thalf), finish(d_txt_out, dt_blk(OWN), 1))
+    ri = Scatter(wi, gi, di_blk, di_half, (ibuf, ihalf), finish(di_blk(OWN), ibuf.at[0], 0))
+    rt = Scatter(wt, gt, dt_blk, dt_half, (tbuf, thalf), finish(dt_blk(OWN), tbuf.at[0], 1))
 
     def hand(k):
         return pltpu.make_async_remote_copy(
@@ -387,14 +406,14 @@
         ref[rows(j), :] += lax.dot_general(gb, img[rows(i), :], (((0,), (0,)), ((), ())), preferred_element_type=F32)
 
     events = {
-        3: [ri.twins],
-        6: [lambda: give_chunk(3)],
-        7: [lambda: take_chunk(3), rt.twins],
-        9: [ri.opposite],
-        11: [lambda: give_chunk(2)],
-        12: [lambda: take_chunk(2), rt.opposite],
-        13: [ri.early],
-        14: [lambda: give_chunk(1)],
+        3: [lambda: give_chunk(3)],
+        4: [lambda: take_chunk(3), rt.twins],
+        6: [ri.twins],
+        9: [lambda: give_chunk(2)],
+        10: [lambda: take_chunk(2), rt.opposite],
+        11: [ri.opposite],
+        13: [lambda: give_chunk(1)],
+        14: [lambda: take_chunk(1), rt.early, ri.early],
     }
     score(0, 0)
     score(0, 1)
@@ -422,26 +441,35 @@
     products(15, 0)
     give_chunk(0)
     products(15, 1)
+    rt.across()
+    ri.twin()
     ri.across()
-    take_chunk(1)
-    rt.early()
-    ri.twin()
+    keep = [pltpu.make_async_copy(x.at[:, half_of(c, n)], img.at[pl.ds((2 + k) * block, block), pl.ds(0, n)], local.at[2 + k]) for k, (x, n) in enumerate(((img_x, img_f), (txt_x, txt_f)))]
+    keep += [pltpu.make_async_copy(img_raw, ibuf.at[0], local.at[0]), pltpu.make_async_copy(txt_raw, tbuf.at[0], local.at[1])]
+    for copy in keep:
+        copy.start()
     take_chunk(0)
     rt.twin()
-    rt.across()
+    for copy in keep:
+        copy.wait()
+    put(img.at[pl.ds(2 * block, block)], 0, img_f, 2)
+    put(img.at[pl.ds(3 * block, block), pl.ds(0, txt_f)], img_f, txt_f, 3)
+    rt.ring()
     ri.ring()
-    rt.ring()
+    rt.last()
     ri.last()
-    rt.last()
+    for k, first in enumerate((feats, feats + img_f)):
+        core.got(8 + k, pack.at[:, pl.ds(first, (img_f, txt_f)[k])], partner)
+        core.got(10 + k, du_view(1, k), partner)
     for k in range(4):
         hand(k).wait_send()
     for copy in outs:
         copy.wait()
-    wi.drain()
-    wt.drain()
-
-
-def main_call(scal, img_emb, txt_emb, img_x, txt_x):
+    for wire in (wi, wt, core):
+        wire.drain()
+
+
+def main_call(scal, img_emb, txt_emb, img_x, txt_x, img_raw, txt_raw):
     block, dim = img_emb.shape
     vmem = pl.BlockSpec(memory_space=pltpu.VMEM)
     hbm = pl.BlockSpec(memory_space=pl.ANY)
@@ -449,13 +477,11 @@
     f = lambda *s: pltpu.VMEM(s, F32)
     return pl.pallas_call(
         functools.partial(main_kernel, block),
-        in_specs=[pl.BlockSpec(memory_space=pltpu.SMEM), hbm, hbm, hbm, hbm],
-        out_specs=[hbm, hbm, vmem, hbm],
+        in_specs=[pl.BlockSpec(memory_space=pltpu.SMEM)] + [hbm] * 6,
+        out_specs=[vmem, hbm],
         out_shape=[
-            jax.ShapeDtypeStruct((block, dim), F32),
-            jax.ShapeDtypeStruct((block, dim), F32),
             jax.ShapeDtypeStruct((3, 8, 128), F32),
-            jax.ShapeDtypeStruct((block, (img_x.shape[1] + txt_x.shape[1]) // 2), BF16),
+            jax.ShapeDtypeStruct((block, img_x.shape[1] + txt_x.shape[1] + 4 * dim), BF16),
         ],
         scratch_shapes=[
             pltpu.VMEM((8 * block, dim), BF16),
@@ -472,11 +498,11 @@
             f(2, block // 2, dim),
             sem((GATHER_COPIES,)), sem((GATHER_COPIES,)), sem((GATHER_COPIES,)), sem((GATHER_COPIES,)),
             sem((SCATTER_COPIES,)), sem((SCATTER_COPIES,)), sem((SCATTER_COPIES,)), sem((SCATTER_COPIES,)),
-            sem((10,)), sem((10,)), sem((4,)), sem((4,)), sem((2,)), pltpu.SemaphoreType.REGULAR,
+            sem((12,)), sem((12,)), sem((4,)), sem((4,)), sem((8,)), pltpu.SemaphoreType.REGULAR,
         ],
         compiler_params=pltpu.CompilerParams(collective_id=0, has_side_effects=True, vmem_limit_bytes=VMEM_LIMIT),
         name="scores",
-    )(scal, img_emb, txt_emb, img_x, txt_x)
+    )(scal, img_emb, txt_emb, img_x, txt_x, img_raw, txt_raw)
 
 
 def pull_back(raw, cot):
@@ -489,18 +515,14 @@
 
 
 def sum_kernel(
-    scal, img_x, txt_x, x_got, img_raw, txt_raw, d_img, d_txt, sums_in, d_w_img, d_w_txt, sums,
-    w, w2, du_own, du, buf1, half1, buf2, half2, small,
-    du_s, du_r, sc_s, sc_r, ga_s, ga_r, out_s, out_r, core_s, core_r, small_s, small_r, local,
+    pack, sums_in, d_w_img, d_w_txt, sums,
+    w, w2, buf1, half1, buf2, half2, small,
+    sc_s, sc_r, ga_s, ga_r, out_s, out_r, core_s, core_r, small_s, small_r, local,
 ):
     place = Place()
     c, partner = place.c, place.partner()
-    du_own[0] = pull_back(img_raw[...], scal[2] * d_img[...])
-    du_own[1] = pull_back(txt_raw[...], scal[2] * d_txt[...])
     greet(place)
-    pre = Wire(du_s, du_r)
-    pre.go(0, du_own, du, partner)
-    img_f, txt_f = img_x.shape[1] // 2, txt_x.shape[1] // 2
+    img_f, txt_f, feats = d_w_img.shape[0] // 2, d_w_txt.shape[0] // 2, w.shape[0]
     ni, nt = img_f // 16, txt_f // 16
     rows, wide = ni + nt, w.shape[1] // 2
     tall, lanes, cut = rows // 2, wide // 4, half2.shape[2]
@@ -508,29 +530,19 @@
     def outer(lhs, rhs):
         return lax.dot_general(lhs, rhs, (((0,), (0,)), ((), ())), preferred_element_type=F32)
 
-    def put(first, size, shift, val, fresh):
-        for b in range(val.shape[0] // size):
-            at = (first // size + b) * rows + shift
-            piece = val[b * size : (b + 1) * size]
-            if fresh:
-                w[at : at + size] = piece
-            else:
-                w[at : at + size] += piece
-
-    def weights(own):
-        rhs = du_own if own else du
-        lane = 128
-        for k in range(0, img_f, lane):
-            cols = pl.ds(pl.multiple_of(c * img_f + k, lane), lane)
-            put(k, ni, 0, outer(img_x[:, cols] if own else x_got[:, k : k + lane], rhs[0]), own)
-        for k in range(0, txt_f, lane):
-            cols = pl.ds(pl.multiple_of(c * txt_f + k, lane), lane)
-            put(k, nt, ni, outer(txt_x[:, cols] if own else x_got[:, img_f + k : img_f + k + lane], rhs[1]), own)
-
-    weights(True)
-    pre.got(0, du, partner)
-    weights(False)
-    pre.drain()
+    def weights(first, count, size, shift, k):
+        lane, dim = 128, w.shape[1]
+        for at in range(0, count, lane):
+            val = sum(
+                outer(pack[:, side * feats + first + at : side * feats + first + at + lane], pack[:, 2 * feats + (2 * side + k) * dim : 2 * feats + (2 * side + k + 1) * dim])
+                for side in range(2)
+            )
+            for b in range(lane // size):
+                to = (at // size + b) * rows + shift
+                w[to : to + size] = val[b * size : (b + 1) * size]
+
+    weights(0, img_f, ni, 0, 0)
+    weights(img_f, txt_f, nt, ni, 1)
 
     small_wire = Wire(small_s, small_r)
     hops = []
@@ -655,9 +667,8 @@
     small_wire.drain()
 
 
-def sum_call(scal, img_x, txt_x, x_got, img_raw, txt_raw, d_img, d_txt, sums):
-    block, feats = x_got.shape
-    dim = d_img.shape[1]
+def sum_call(pack, sums, img_x, txt_x, dim):
+    feats = (img_x.shape[1] + txt_x.shape[1]) // 2
     vmem = pl.BlockSpec(memory_space=pltpu.VMEM)
     hbm = pl.BlockSpec(memory_space=pl.ANY)
     sem = lambda n: [pltpu.SemaphoreType.DMA((n,))] * 2
@@ -666,7 +677,7 @@
     tall, lanes, cut = rows // 2, wide // 4, 24
     return pl.pallas_call(
         sum_kernel,
-        in_specs=[pl.BlockSpec(memory_space=pltpu.SMEM)] + [vmem] * 8,
+        in_specs=[vmem, vmem],
         out_specs=[hbm, hbm, vmem],
         out_shape=[
             jax.ShapeDtypeStruct((img_x.shape[1], dim), F32),
@@ -676,17 +687,15 @@
         scratch_shapes=[
             f(feats, dim),
             f(2 * rows, dim),
-            pltpu.VMEM((2, block, dim), BF16),
-            pltpu.VMEM((2, block, dim), BF16),
             f(COLOURS, 6, rows, wide), f(COLOURS, 2, tall, wide),
             f(COLOURS, 6, tall, lanes), f(COLOURS, 2, cut, lanes),
             f(15, *sums.shape),
-            *sem(1), *sem(2 * COLOURS * SCATTER_COPIES), *sem(COLOURS * GATHER_COPIES), *sem(2 * COLOURS * GATHER_COPIES),
+            *sem(2 * COLOURS * SCATTER_COPIES), *sem(COLOURS * GATHER_COPIES), *sem(2 * COLOURS * GATHER_COPIES),
             *sem(2 * COLOURS * 8), *sem(7), pltpu.SemaphoreType.DMA((2 * COLOURS,)),
         ],
         compiler_params=pltpu.CompilerParams(collective_id=1, has_side_effects=True, vmem_limit_bytes=32 * 2**20),
         name="weights",
-    )(scal, img_x, txt_x, x_got, img_raw, txt_raw, d_img, d_txt, sums)
+    )(pack, sums)
 
 
 def store_kernel(total_rows, scal, sums, src_a, src_b, loss, d_temp, d_bias, dst_a, dst_b, sems):
@@ -726,8 +735,8 @@
         img_raw, img_emb = embed_rows(img_x, w_img)
         temp_scale = jnp.exp(log_temp[0])
         scal = jnp.stack([temp_scale, logit_bias[0], temp_scale / total_rows])
-        d_img, d_txt, sums, x_got = main_call(scal, img_emb, txt_emb, img_x, txt_x)
-        d_w_img, d_w_txt, sums = sum_call(scal, img_x, txt_x, x_got, img_raw, txt_raw, d_img, d_txt, sums)
+        sums, pack = main_call(scal, img_emb, txt_emb, img_x, txt_x, img_raw, txt_raw)
+        d_w_img, d_w_txt, sums = sum_call(pack, sums, img_x, txt_x, w_img.shape[1])
         return tuple(store_call(total_rows, scal, sums, d_w_img, d_w_txt))
 
     batch_spec = P(batch_axes, None)

time: 265 us -> 253 us (0.955)
  local copies, waits for them, and re-layouts: 10.5 us -> 4.3 us
  Pallas kernels: 245 us -> 240 us
    unnamed x26 -> x14, local copies, waits for them, and re-layouts: 10.5 us -> 4.29 us
    pallas_call x1, Pallas kernels: 79.4 us -> 74.3 us  [sum_call(): pl.pallas_call(sum_kernel, in_specs=[vmem, vmem], out_specs=[hbm, hbm, vm...]
where the time goes in v5:
time: 253 us
  Pallas kernels  240 us (95%)
  matrix products  4.36 us (2%)
  local copies, waits for them, and re-layouts  4.3 us (2%)
    pallas_call x1, Pallas kernels, main_call(): pl.pallas_call(functools.partial(main_kernel, block), in_specs=[pl.BlockS...  160 us
    pallas_call x1, Pallas kernels, sum_call(): pl.pallas_call(sum_kernel, in_specs=[vmem, vmem], out_specs=[hbm, hbm, vm...  74.3 us
    pallas_call x1, Pallas kernels, store_call(): pl.pallas_call(functools.partial(store_kernel, total_rows), in_specs=[sme...  5.17 us

profile of v5, /device:TPU:1, one launch (start us, length us, event | category | flops | bytes accessed | tf_op | source)
XLA Modules:
  0.0 252.6 jit_solution(10016256155817439071)
XLA Ops:
  0.6 0.0 copy-start.5
  0.6 0.0 copy-start.6
  2.1 0.6 pad_maximum_fusion.scal
  2.7 3.8 %multiply_reduce_fusion.1 = (f32[256]{0:T(256)S(1)}, f32[256,1024]{1,0:T(8,128)S(1)}) fusion(bf16[256,2048]{1,0:T(8,128)(2,1)} %img_x.1, bf16[2048,1024]{1,0:T(8,128)(2,1)} %param.8), kind=kOutput, calls=%fused_computation.3 | convolution fusion | flops 1074265856 | bytes 6292480 | tf_op jit(solution)/shard_map/dot_general | solution.py:18
  6.5 0.0 copy-start.4
  6.5 0.0 copy-done.5
  6.5 0.0 copy-done.6
  6.6 0.5 multiply_reduce_fusion
  7.1 0.0 copy-start.3
  7.1 1.0 copy-done.3
  8.1 1.2 multiply_convert_fusion
  9.2 0.0 copy-done.4
  9.2 160.4 %scores.1 = (f32[3,8,128]{2,1,0:T(8,128)}, bf16[256,6656]{1,0:T(8,128)(2,1)}) custom-call(f32[3]{0:T(128)} %pad_maximum_fusion.scal, bf16[256,1024]{1,0:T(8,128)(2,1)} %get-tuple-element.20.img_own, bf16[256,1024]{1,0:T(8,128)(2,1)} %get-tuple-element.19.txt_own, bf16[256,2048]{1,0:T(8,128)(2,1)} %img_x.1, bf16[256,512]{1,0:T(8,128)(2,1)} %txt_x.1, ...), custom_call_target="tpu_custom_call" | custom-call | tf_op jit(solution)/shard_map/scores/pallas_call | solution.py:478
  169.6 0.0 copy-start
  169.6 2.0 copy-done
  171.6 0.0 copy-start.1
  171.6 0.7 copy-done.1
  172.3 74.3 %weights.1 = (f32[2048,1024]{1,0:T(8,128)S(1)}, f32[512,1024]{1,0:T(8,128)S(1)}, f32[3,8,128]{2,1,0:T(8,128)S(1)}) custom-call(bf16[256,6656]{1,0:T(8,128)(2,1)S(1)} %copy-done, f32[3,8,128]{2,1,0:T(8,128)S(1)} %copy-done.1), custom_call_target="tpu_custom_call" | custom-call | tf_op jit(solution)/shard_map/weights/pallas_call | solution.py:678
  246.6 0.0 copy-start.2
  246.6 0.6 copy-done.2
  247.2 5.2 %store.1 = (f32[1]{0:T(128)}, f32[1]{0:T(128)}, f32[1]{0:T(128)}, f32[2048,1024]{1,0:T(8,128)}, f32[512,1024]{1,0:T(8,128)}) custom-call(f32[3]{0:T(128)S(1)} %copy-done.2, f32[3,8,128]{2,1,0:T(8,128)S(1)} %get-tuple-element.12.sums, f32[2048,1024]{1,0:T(8,128)S(1)} %get-tuple-element.13.src_a, f32[512,1024]{1,0:T(8,128)S(1)} %get-tuple-element.14.src_b), custom_call_target="tpu_custom_call" | custom-call | tf_op jit(solution)/shard_map/store/pallas_call | solution.py:716
  (2 shorter events, 0.0 us)
Async XLA Ops:
  0.6 5.9 %copy-start.5 = (bf16[256,512]{1,0:T(8,128)(2,1)S(1)}, bf16[256,512]{1,0:T(8,128)(2,1)}, u32[]{:S(2)}) copy-start(bf16[256,512]{1,0:T(8,128)(2,1)} %txt_x.1) | copy-start | bytes 786436
  0.6 5.9 %copy-start.6 = (bf16[512,1024]{1,0:T(8,128)(2,1)S(1)}, bf16[512,1024]{1,0:T(8,128)(2,1)}, u32[]{:S(2)}) copy-start(bf16[512,1024]{1,0:T(8,128)(2,1)} %param.9) | copy-start | bytes 3145732
  6.5 2.7 %copy-start.4 = (f32[256,1024]{1,0:T(8,128)}, f32[256,1024]{1,0:T(8,128)S(1)}, u32[]{:S(2)}) copy-start(f32[256,1024]{1,0:T(8,128)S(1)} %get-tuple-element.16.img_raw) | copy-start | bytes 3145732
  7.1 1.0 copy-start.3
  169.6 2.0 copy-start
  171.6 0.7 copy-start.1
  246.6 0.7 copy-start.2

commit v6 on v5

--- a/solution.py
+++ b/solution.py
@@ -19,6 +19,11 @@
     return raw, (raw * lax.rsqrt(jnp.sum(raw * raw, axis=-1, keepdims=True))).astype(BF16)
 
 
+OWN, RIGHT, LEFT, FAR = ((0, step) for step in (0, 1, -1, 2))
+TWIN, TWIN_RIGHT, TWIN_LEFT, TWIN_FAR = ((1, step) for step in (0, 1, -1, 2))
+SEEN = [OWN, LEFT, RIGHT, TWIN, FAR, TWIN_LEFT, TWIN_RIGHT, TWIN_FAR]
+
+
 class Place:
     def __init__(self):
         rep, dat = lax.axis_index("replica"), lax.axis_index("data")
@@ -42,30 +47,28 @@
         return v - 1 + 2 * lax.rem(v, 2)
 
     def image_group(self):
-        return Group(self.x, lax.rem(lax.div(self.y + 1, 2), 2), self.at(x=self.x + 1), self.at(x=self.x - 1), self.at(y=self.near(self.y)))
+        return Group(self.x, lax.rem(lax.div(self.y + 1, 2), 2), lambda key: self.at(x=self.x + key[1], y=self.near(self.y) if key[0] else None))
 
     def text_group(self):
-        return Group(self.z, lax.div(self.y, 2), self.at(z=self.z + 1), self.at(z=self.z - 1), self.at(y=self.far(self.y)))
-
-    def peers(self):
-        out = [self.partner()]
-        for g in (self.image_group(), self.text_group()):
-            out += [g.right, g.left, g.pair]
-        return out
+        return Group(self.z, lax.div(self.y, 2), lambda key: self.at(z=self.z + key[1], y=self.far(self.y) if key[0] else None))
+
+    def peers(self, keys):
+        return [self.partner()] + [g.dev(key) for g in (self.image_group(), self.text_group()) for key in keys]
 
 
 class Group:
-    def __init__(self, pos, side, right, left, pair):
-        self.pos, self.side, self.right, self.left, self.pair = pos, side, right, left, pair
+    def __init__(self, pos, side, dev):
+        self.pos, self.side, self.dev = pos, side, dev
+        self.right, self.left, self.pair = (dev(key) for key in (RIGHT, LEFT, TWIN))
 
     def slot(self, key):
         side = 1 - self.side if key[0] else self.side
         return side * 4 + lax.rem(self.pos + key[1] + 4, 4)
 
 
-def greet(place):
+def greet(place, keys):
     barrier = pltpu.get_barrier_semaphore()
-    peers = place.peers()
+    peers = place.peers(keys)
     for dev in peers:
         pl.semaphore_signal(barrier, inc=1, device_id=dev, device_id_type=MESH)
     pl.semaphore_wait(barrier, len(peers))
@@ -110,8 +113,6 @@
 
 GATHER_COPIES = 8
 SCATTER_COPIES = 10
-OWN, RIGHT, LEFT, FAR = ((0, step) for step in (0, 1, -1, 2))
-TWIN, TWIN_RIGHT, TWIN_LEFT, TWIN_FAR = ((1, step) for step in (0, 1, -1, 2))
 
 
 def gather_stages(wire, g, own, blk, half, relative, seen=None):
@@ -164,7 +165,30 @@
     return [start, ring, twin, across, last]
 
 
-SEEN = [OWN, LEFT, RIGHT, TWIN, FAR, TWIN_LEFT, TWIN_RIGHT, TWIN_FAR]
+def direct_stages(wire, g, blk):
+    def send():
+        for k, key in enumerate(SEEN[1:]):
+            wire.go(k, blk(OWN), blk(OWN), g.dev(key))
+
+    def take():
+        for k, (twin, step) in enumerate(SEEN[1:]):
+            back = (twin, step if step == 2 else -step)
+            wire.got(k, blk(back), g.dev(back))
+
+    return [send, take]
+
+
+def direct_scatter_stages(wire, g, blk, bufs, done):
+    def send():
+        for k, key in enumerate(SEEN[1:]):
+            wire.go(k, blk(key), bufs.at[k], g.dev(key))
+
+    def take():
+        for k, (twin, step) in enumerate(SEEN[1:]):
+            wire.got(k, bufs.at[k], g.dev((twin, step if step == 2 else -step)))
+        done([bufs[k] for k in range(7)])
+
+    return [send, take]
 
 
 class Scatter:
@@ -287,7 +311,7 @@
     gi, gt = place.image_group(), place.text_group()
     c = place.c
     partner = place.partner()
-    greet(place)
+    greet(place, (RIGHT, LEFT, TWIN))
 
     half_rows = 8 * block
     img_blk, img_half = rows_of(img, block)
@@ -516,33 +540,36 @@
 
 def sum_kernel(
     pack, sums_in, d_w_img, d_w_txt, sums,
-    w, w2, buf1, half1, buf2, half2, small,
+    w, w2, buf1, half1, buf2, small,
     sc_s, sc_r, ga_s, ga_r, out_s, out_r, core_s, core_r, small_s, small_r, local,
 ):
     place = Place()
     c, partner = place.c, place.partner()
-    greet(place)
+    greet(place, SEEN[1:])
     img_f, txt_f, feats = d_w_img.shape[0] // 2, d_w_txt.shape[0] // 2, w.shape[0]
     ni, nt = img_f // 16, txt_f // 16
     rows, wide = ni + nt, w.shape[1] // 2
-    tall, lanes, cut = rows // 2, wide // 4, half2.shape[2]
+    tall, lanes = rows // 2, wide // 4
 
     def outer(lhs, rhs):
         return lax.dot_general(lhs, rhs, (((0,), (0,)), ((), ())), preferred_element_type=F32)
 
-    def weights(first, count, size, shift, k):
+    def weights(to, first, count, size, shift, k):
         lane, dim = 128, w.shape[1]
         for at in range(0, count, lane):
             val = sum(
-                outer(pack[:, side * feats + first + at : side * feats + first + at + lane], pack[:, 2 * feats + (2 * side + k) * dim : 2 * feats + (2 * side + k + 1) * dim])
+                outer(pack[:, side * feats + first + at : side * feats + first + at + lane], pack[:, pl.ds(2 * feats + (2 * side + k) * dim + to * wide, wide)])
                 for side in range(2)
             )
             for b in range(lane // size):
-                to = (at // size + b) * rows + shift
-                w[to : to + size] = val[b * size : (b + 1) * size]
-
-    weights(0, img_f, ni, 0, 0)
-    weights(img_f, txt_f, nt, ni, 1)
+                top = (at // size + b) * rows + shift
+                w[top : top + size, pl.ds(to * wide, wide)] = val[b * size : (b + 1) * size]
+
+    def lane_half(to):
+        weights(to, 0, img_f, ni, 0, 0)
+        weights(to, img_f, txt_f, nt, ni, 1)
+
+    lane_half(0)
 
     small_wire = Wire(small_s, small_r)
     hops = []
@@ -593,11 +620,7 @@
                 top, cols = at(key)
                 return ref.at[rows_at(top, tall), cols]
 
-            def half(key, h):
-                top, cols = at(key)
-                return ref.at[rows_at(top + h * cut, tall - cut if h else cut), cols]
-
-            return blk, half
+            return blk
 
         def outs(key, core, h, parts):
             at = group + g1.slot(key)
@@ -613,16 +636,16 @@
         def o_half(key, h):
             return outs(key, c, h, 2)
 
-        ws_blk, ws_half = strip(w, mine)
-        os_blk, os_half = strip(w2, keep)
+        ws_blk = strip(w, mine)
+        os_blk = strip(w2, keep)
 
         def done1(p, q, r):
             v = w_blk(OWN)
             v[...] += p[...] + q[...] + r[...]
 
-        def done2(p, q, r):
+        def done2(terms):
             v = os_blk(OWN)
-            v[...] = ws_blk(OWN)[...] + p[...] + q[...] + r[...]
+            v[...] = ws_blk(OWN)[...] + sum(terms)
 
         whole = w2.at[pl.ds(keep, ni), across], w2.at[pl.ds(keep + ni, nt), across]
         turn = iter(range(n * 8, n * 8 + 8))
@@ -644,8 +667,8 @@
         w1, w2_, w3 = (Wire(*args) for args in ((sc_s, sc_r, n * SCATTER_COPIES), (sc_s, sc_r, (COLOURS + n) * SCATTER_COPIES), (ga_s, ga_r, n * GATHER_COPIES)))
         w4 = Pieces(out_s, out_r, 2 * n * GATHER_COPIES)
         stages = Scatter(w1, g1, w_blk, w_half, (buf1.at[n], half1.at[n]), done1).stages()
-        stages += Scatter(w2_, g2, ws_blk, ws_half, (buf2.at[n], half2.at[n]), done2).stages()
-        stages += gather_stages(w3, g2, os_blk(OWN), os_blk, os_half, False)
+        stages += direct_scatter_stages(w2_, g2, ws_blk, buf2.at[n], done2)
+        stages += direct_stages(w3, g2, os_blk)
         tail = gather_stages(w4, g1, whole, o_blk, o_half, False, share)
         stages += [tail[0], share_own] + tail[1:] + [got_shares]
         return stages, [w1, w2_, w3, w4]
@@ -653,9 +676,11 @@
     colours = [colour(n) for n in range(COLOURS)]
     for n in range(len(colours[0][0]) + 1):
         for k, (stages, _) in enumerate(colours):
-            at = n - k // 2
+            at = n - k // 2 * 1
             if 0 <= at < len(stages):
                 stages[at]()
+        if n == 0:
+            lane_half(1)
         small_step(n)
     sums[...] = small[2 * len(hops)]
     for copy in copies:
@@ -674,7 +699,7 @@
     sem = lambda n: [pltpu.SemaphoreType.DMA((n,))] * 2
     f = lambda *s: pltpu.VMEM(s, F32)
     rows, wide = feats // 16, dim // 2
-    tall, lanes, cut = rows // 2, wide // 4, 24
+    tall, lanes = rows // 2, wide // 4
     return pl.pallas_call(
         sum_kernel,
         in_specs=[vmem, vmem],
@@ -688,7 +713,7 @@
             f(feats, dim),
             f(2 * rows, dim),
             f(COLOURS, 6, rows, wide), f(COLOURS, 2, tall, wide),
-            f(COLOURS, 6, tall, lanes), f(COLOURS, 2, cut, lanes),
+            f(COLOURS, 7, tall, lanes),
             f(15, *sums.shape),
             *sem(2 * COLOURS * SCATTER_COPIES), *sem(COLOURS * GATHER_COPIES), *sem(2 * COLOURS * GATHER_COPIES),
             *sem(2 * COLOURS * 8), *sem(7), pltpu.SemaphoreType.DMA((2 * COLOURS,)),

time: 253 us -> 247 us (0.976)
  Pallas kernels: 240 us -> 234 us
    pallas_call x1, Pallas kernels: 74.3 us -> 68.1 us  [sum_call(): pl.pallas_call(sum_kernel, in_specs=[vmem, vmem], out_specs=[hbm, hbm, vm...]
where the time goes in v6:
time: 247 us; the launch traced here: 246 us
  Pallas kernels  234 us (95%)
  matrix products  4.36 us (2%)
  local copies, waits for them, and re-layouts  4.3 us (2%)
    pallas_call x1, Pallas kernels, main_call(): pl.pallas_call(functools.partial(main_kernel, block), in_specs=[pl.BlockS...  160 us
    pallas_call x1, Pallas kernels, sum_call(): pl.pallas_call(sum_kernel, in_specs=[vmem, vmem], out_specs=[hbm, hbm, vm...  68.1 us
    pallas_call x1, Pallas kernels, store_call(): pl.pallas_call(functools.partial(store_kernel, total_rows), in_specs=[sme...  5.17 us

profile of v6, /device:TPU:1, one launch (start us, length us, event | category | flops | bytes accessed | tf_op | source)
XLA Modules:
  0.0 246.4 jit_solution(74455782590553503)
XLA Ops:
  0.6 0.0 copy-start.5
  0.6 0.0 copy-start.6
  2.1 0.6 pad_maximum_fusion.scal
  2.7 3.8 %multiply_reduce_fusion.1 = (f32[256]{0:T(256)S(1)}, f32[256,1024]{1,0:T(8,128)S(1)}) fusion(bf16[256,2048]{1,0:T(8,128)(2,1)} %img_x.1, bf16[2048,1024]{1,0:T(8,128)(2,1)} %param.8), kind=kOutput, calls=%fused_computation.3 | convolution fusion | flops 1074265856 | bytes 6292480 | tf_op jit(solution)/shard_map/dot_general | solution.py:18
  6.5 0.0 copy-start.4
  6.5 0.0 copy-done.5
  6.5 0.0 copy-done.6
  6.6 0.5 multiply_reduce_fusion
  7.1 0.0 copy-start.3
  7.1 1.0 copy-done.3
  8.1 1.2 multiply_convert_fusion
  9.2 0.0 copy-done.4
  9.2 160.5 %scores.1 = (f32[3,8,128]{2,1,0:T(8,128)}, bf16[256,6656]{1,0:T(8,128)(2,1)}) custom-call(f32[3]{0:T(128)} %pad_maximum_fusion.scal, bf16[256,1024]{1,0:T(8,128)(2,1)} %get-tuple-element.20.img_own, bf16[256,1024]{1,0:T(8,128)(2,1)} %get-tuple-element.19.txt_own, bf16[256,2048]{1,0:T(8,128)(2,1)} %img_x.1, bf16[256,512]{1,0:T(8,128)(2,1)} %txt_x.1, ...), custom_call_target="tpu_custom_call" | custom-call | tf_op jit(solution)/shard_map/scores/pallas_call | solution.py:502
  169.7 0.0 copy-start
  169.7 2.0 copy-done
  171.6 0.0 copy-start.1
  171.6 0.7 copy-done.1
  172.3 68.1 %weights.1 = (f32[2048,1024]{1,0:T(8,128)S(1)}, f32[512,1024]{1,0:T(8,128)S(1)}, f32[3,8,128]{2,1,0:T(8,128)S(1)}) custom-call(bf16[256,6656]{1,0:T(8,128)(2,1)S(1)} %copy-done, f32[3,8,128]{2,1,0:T(8,128)S(1)} %copy-done.1), custom_call_target="tpu_custom_call" | custom-call | tf_op jit(solution)/shard_map/weights/pallas_call | solution.py:703
  240.4 0.0 copy-start.2
  240.4 0.6 copy-done.2
  241.1 5.2 %store.1 = (f32[1]{0:T(128)}, f32[1]{0:T(128)}, f32[1]{0:T(128)}, f32[2048,1024]{1,0:T(8,128)}, f32[512,1024]{1,0:T(8,128)}) custom-call(f32[3]{0:T(128)S(1)} %copy-done.2, f32[3,8,128]{2,1,0:T(8,128)S(1)} %get-tuple-element.12.sums, f32[2048,1024]{1,0:T(8,128)S(1)} %get-tuple-element.13.src_a, f32[512,1024]{1,0:T(8,128)S(1)} %get-tuple-element.14.src_b), custom_call_target="tpu_custom_call" | custom-call | tf_op jit(solution)/shard_map/store/pallas_call | solution.py:741
  (2 shorter events, 0.0 us)
Async XLA Ops:
  0.6 5.9 %copy-start.5 = (bf16[256,512]{1,0:T(8,128)(2,1)S(1)}, bf16[256,512]{1,0:T(8,128)(2,1)}, u32[]{:S(2)}) copy-start(bf16[256,512]{1,0:T(8,128)(2,1)} %txt_x.1) | copy-start | bytes 786436
  0.6 5.9 %copy-start.6 = (bf16[512,1024]{1,0:T(8,128)(2,1)S(1)}, bf16[512,1024]{1,0:T(8,128)(2,1)}, u32[]{:S(2)}) copy-start(bf16[512,1024]{1,0:T(8,128)(2,1)} %param.9) | copy-start | bytes 3145732
  6.5 2.7 %copy-start.4 = (f32[256,1024]{1,0:T(8,128)}, f32[256,1024]{1,0:T(8,128)S(1)}, u32[]{:S(2)}) copy-start(f32[256,1024]{1,0:T(8,128)S(1)} %get-tuple-element.16.img_raw) | copy-start | bytes 3145732
  7.1 1.0 copy-start.3
  169.7 2.0 copy-start
  171.6 0.7 copy-start.1
  240.4 0.7 copy-start.2

commit v7 on v6

--- a/solution.py
+++ b/solution.py
@@ -159,10 +159,12 @@
         wire.got(6, blk(TWIN_RIGHT), g.right)
         seen(TWIN_LEFT)
         seen(TWIN_RIGHT)
+
+    def far():
         wire.got(7, blk(TWIN_FAR), g.pair)
         seen(TWIN_FAR)
 
-    return [start, ring, twin, across, last]
+    return [start, ring, twin, across, last, far]
 
 
 def direct_stages(wire, g, blk):
@@ -345,11 +347,19 @@
     core.go(9, txt_x.at[:, half_of(1 - c, txt_f)], pack.at[:, pl.ds(feats + img_f, txt_f)], partner)
     for ref in (d_img, d_txt, give, sums):
         ref[...] = jnp.zeros_like(ref)
-    run_both(a[1:], b[1:])
-    for k, key in enumerate(SEEN):
-        core.got(k, other_blk(key), partner)
-    wi.drain()
-    wt.drain()
+    run_both(a[1:4], b[1:4])
+    b[4]()
+
+    def take_texts(first, last):
+        for k in range(first, last):
+            core.got(k, other_blk(SEEN[k]), partner)
+
+    def gather_rest():
+        b[5]()
+        a[4]()
+        a[5]()
+
+    take_texts(0, 7)
 
     scale, bias = scal[0], scal[1]
     di_blk, di_half = rows_of(d_img, block)
@@ -382,9 +392,9 @@
 
         return done
 
-    wi, wt = Wire(is_s, is_r), Wire(ts_s, ts_r)
-    ri = Scatter(wi, gi, di_blk, di_half, (ibuf, ihalf), finish(di_blk(OWN), ibuf.at[0], 0))
-    rt = Scatter(wt, gt, dt_blk, dt_half, (tbuf, thalf), finish(dt_blk(OWN), tbuf.at[0], 1))
+    si, st = Wire(is_s, is_r), Wire(ts_s, ts_r)
+    ri = Scatter(si, gi, di_blk, di_half, (ibuf, ihalf), finish(di_blk(OWN), ibuf.at[0], 0))
+    rt = Scatter(st, gt, dt_blk, dt_half, (tbuf, thalf), finish(dt_blk(OWN), tbuf.at[0], 1))
 
     def hand(k):
         return pltpu.make_async_remote_copy(
@@ -430,6 +440,8 @@
         ref[rows(j), :] += lax.dot_general(gb, img[rows(i), :], (((0,), (0,)), ((), ())), preferred_element_type=F32)
 
     events = {
+        0: [gather_rest],
+        2: [lambda: take_texts(7, 8)],
         3: [lambda: give_chunk(3)],
         4: [lambda: take_chunk(3), rt.twins],
         6: [ri.twins],
@@ -468,6 +480,8 @@
     rt.across()
     ri.twin()
     ri.across()
+    wi.drain()
+    wt.drain()
     keep = [pltpu.make_async_copy(x.at[:, half_of(c, n)], img.at[pl.ds((2 + k) * block, block), pl.ds(0, n)], local.at[2 + k]) for k, (x, n) in enumerate(((img_x, img_f), (txt_x, txt_f)))]
     keep += [pltpu.make_async_copy(img_raw, ibuf.at[0], local.at[0]), pltpu.make_async_copy(txt_raw, tbuf.at[0], local.at[1])]
     for copy in keep:
@@ -489,7 +503,7 @@
         hand(k).wait_send()
     for copy in outs:
         copy.wait()
-    for wire in (wi, wt, core):
+    for wire in (si, st, core):
         wire.drain()
 
 

time: 247 us -> 243 us (0.984)
  Pallas kernels: 234 us -> 230 us
where the time goes in v7:
time: 243 us
  Pallas kernels  230 us (95%)
  matrix products  4.36 us (2%)
  local copies, waits for them, and re-layouts  4.3 us (2%)
    pallas_call x1, Pallas kernels, main_call(): pl.pallas_call(functools.partial(main_kernel, block), in_specs=[pl.BlockS...  159 us
    pallas_call x1, Pallas kernels, sum_call(): pl.pallas_call(sum_kernel, in_specs=[vmem, vmem], out_specs=[hbm, hbm, vm...  66.2 us
    pallas_call x1, Pallas kernels, store_call(): pl.pallas_call(functools.partial(store_kernel, total_rows), in_specs=[sme...  5.17 us

profile of v7, /device:TPU:1, one launch (start us, length us, event | category | flops | bytes accessed | tf_op | source)
XLA Modules:
  0.0 243.1 jit_solution(6033734420506485176)
XLA Ops:
  0.6 0.0 copy-start.5
  0.6 0.0 copy-start.6
  2.1 0.6 pad_maximum_fusion.scal
  2.7 3.8 %multiply_reduce_fusion.1 = (f32[256]{0:T(256)S(1)}, f32[256,1024]{1,0:T(8,128)S(1)}) fusion(bf16[256,2048]{1,0:T(8,128)(2,1)} %img_x.1, bf16[2048,1024]{1,0:T(8,128)(2,1)} %param.8), kind=kOutput, calls=%fused_computation.3 | convolution fusion | flops 1074265856 | bytes 6292480 | tf_op jit(solution)/shard_map/dot_general | solution.py:18
  6.5 0.0 copy-start.4
  6.5 0.0 copy-done.5
  6.5 0.0 copy-done.6
  6.6 0.5 multiply_reduce_fusion
  7.1 0.0 copy-start.3
  7.1 1.0 copy-done.3
  8.1 1.2 multiply_convert_fusion
  9.2 0.0 copy-done.4
  9.2 159.0 %scores.1 = (f32[3,8,128]{2,1,0:T(8,128)}, bf16[256,6656]{1,0:T(8,128)(2,1)}) custom-call(f32[3]{0:T(128)} %pad_maximum_fusion.scal, bf16[256,1024]{1,0:T(8,128)(2,1)} %get-tuple-element.20.img_own, bf16[256,1024]{1,0:T(8,128)(2,1)} %get-tuple-element.19.txt_own, bf16[256,2048]{1,0:T(8,128)(2,1)} %img_x.1, bf16[256,512]{1,0:T(8,128)(2,1)} %txt_x.1, ...), custom_call_target="tpu_custom_call" | custom-call | tf_op jit(solution)/shard_map/scores/pallas_call | solution.py:516
  168.3 0.0 copy-start
  168.3 2.0 copy-done
  170.2 0.0 copy-start.1
  170.2 0.7 copy-done.1
  170.9 66.2 %weights.1 = (f32[2048,1024]{1,0:T(8,128)S(1)}, f32[512,1024]{1,0:T(8,128)S(1)}, f32[3,8,128]{2,1,0:T(8,128)S(1)}) custom-call(bf16[256,6656]{1,0:T(8,128)(2,1)S(1)} %copy-done, f32[3,8,128]{2,1,0:T(8,128)S(1)} %copy-done.1), custom_call_target="tpu_custom_call" | custom-call | tf_op jit(solution)/shard_map/weights/pallas_call | solution.py:717
  237.1 0.0 copy-start.2
  237.1 0.6 copy-done.2
  237.8 5.2 %store.1 = (f32[1]{0:T(128)}, f32[1]{0:T(128)}, f32[1]{0:T(128)}, f32[2048,1024]{1,0:T(8,128)}, f32[512,1024]{1,0:T(8,128)}) custom-call(f32[3]{0:T(128)S(1)} %copy-done.2, f32[3,8,128]{2,1,0:T(8,128)S(1)} %get-tuple-element.12.sums, f32[2048,1024]{1,0:T(8,128)S(1)} %get-tuple-element.13.src_a, f32[512,1024]{1,0:T(8,128)S(1)} %get-tuple-element.14.src_b), custom_call_target="tpu_custom_call" | custom-call | tf_op jit(solution)/shard_map/store/pallas_call | solution.py:755
  (2 shorter events, 0.0 us)
Async XLA Ops:
  0.6 5.9 %copy-start.5 = (bf16[256,512]{1,0:T(8,128)(2,1)S(1)}, bf16[256,512]{1,0:T(8,128)(2,1)}, u32[]{:S(2)}) copy-start(bf16[256,512]{1,0:T(8,128)(2,1)} %txt_x.1) | copy-start | bytes 786436
  0.6 5.9 %copy-start.6 = (bf16[512,1024]{1,0:T(8,128)(2,1)S(1)}, bf16[512,1024]{1,0:T(8,128)(2,1)}, u32[]{:S(2)}) copy-start(bf16[512,1024]{1,0:T(8,128)(2,1)} %param.9) | copy-start | bytes 3145732
  6.5 2.7 %copy-start.4 = (f32[256,1024]{1,0:T(8,128)}, f32[256,1024]{1,0:T(8,128)S(1)}, u32[]{:S(2)}) copy-start(f32[256,1024]{1,0:T(8,128)S(1)} %get-tuple-element.16.img_raw) | copy-start | bytes 3145732
  7.1 1.0 copy-start.3
  168.3 2.0 copy-start
  170.2 0.7 copy-start.1
  237.1 0.7 copy-start.2

commit v8 on v7

--- a/solution.py
+++ b/solution.py
@@ -71,7 +71,7 @@
     peers = place.peers(keys)
     for dev in peers:
         pl.semaphore_signal(barrier, inc=1, device_id=dev, device_id_type=MESH)
-    pl.semaphore_wait(barrier, len(peers))
+    return lambda: pl.semaphore_wait(barrier, len(peers))
 
 
 class Wire:
@@ -282,9 +282,10 @@
     if diag is not None:
         z = jnp.where(diag, -z, z)
     e = jnp.exp(-jnp.abs(z))
-    r = 1.0 / (1.0 + e)
+    w = 1.0 + e
+    r = pl.reciprocal(w)
     g = jnp.where(z >= 0.0, r, e * r)
-    loss = jnp.maximum(z, 0.0) + jnp.log1p(e)
+    loss = jnp.maximum(z, 0.0) + jnp.where(e < 1e-4, e * (1.0 - 0.5 * e), jnp.log(w))
     if diag is not None:
         g = jnp.where(diag, -g, g)
     return loss, g
@@ -313,7 +314,7 @@
     gi, gt = place.image_group(), place.text_group()
     c = place.c
     partner = place.partner()
-    greet(place, (RIGHT, LEFT, TWIN))
+    met = greet(place, (RIGHT, LEFT, TWIN))
 
     half_rows = 8 * block
     img_blk, img_half = rows_of(img, block)
@@ -327,6 +328,7 @@
     own_t.start()
     own_i.wait()
     own_t.wait()
+    met()
     sent = iter(range(8))
 
     def share(key):
@@ -424,13 +426,21 @@
         i, j = tile_of(m)
         sbuf[cc] = lax.dot_general(img[rows(i), :], txt[txt_rows(cc, j), :], (((1,), (1,)), ((), ())), preferred_element_type=F32)
 
-    def point(cc, diag=None):
-        sim = sbuf[cc]
+    def part_of_point(cc, at, diag=None):
+        sim = sbuf[cc, at]
         loss, g = score_terms(sim, scale, bias, diag)
         sums[0] += fold(loss)
         sums[1] += fold(g * sim)
         sums[2] += fold(g)
-        gbuf[cc] = g.astype(BF16)
+        gbuf[cc, at] = g.astype(BF16)
+
+    def point(cc, diag=None):
+        if diag is None:
+            part_of_point(cc, slice(0, block))
+            part_of_point(cc, slice(block, TILE))
+        else:
+            part_of_point(cc, slice(0, block), diag)
+            part_of_point(cc, slice(block, TILE))
 
     def products(m, cc):
         i, j = tile_of(m)
@@ -471,9 +481,9 @@
         return carry
 
     lax.fori_loop(0, 15, step, 0)
-    row = lax.broadcasted_iota(jnp.int32, (TILE, TILE), 0)
-    col = lax.broadcasted_iota(jnp.int32, (TILE, TILE), 1)
-    point(1, (row == col) & (row < block))
+    row = lax.broadcasted_iota(jnp.int32, (block, TILE), 0)
+    col = lax.broadcasted_iota(jnp.int32, (block, TILE), 1)
+    point(1, row == col)
     products(15, 0)
     give_chunk(0)
     products(15, 1)
@@ -559,7 +569,7 @@
 ):
     place = Place()
     c, partner = place.c, place.partner()
-    greet(place, SEEN[1:])
+    met = greet(place, SEEN[1:])
     img_f, txt_f, feats = d_w_img.shape[0] // 2, d_w_txt.shape[0] // 2, w.shape[0]
     ni, nt = img_f // 16, txt_f // 16
     rows, wide = ni + nt, w.shape[1] // 2
@@ -584,6 +594,7 @@
         weights(to, img_f, txt_f, nt, ni, 1)
 
     lane_half(0)
+    met()
 
     small_wire = Wire(small_s, small_r)
     hops = []

time: 243 us -> 239 us (0.984)
  Pallas kernels: 230 us -> 226 us
    pallas_call x1, Pallas kernels: 159 us -> 155 us  [main_call(): pl.pallas_call(functools.partial(main_kernel, block), in_specs=[pl.BlockS...]
where the time goes in v8:
time: 239 us
  Pallas kernels  226 us (95%)
  matrix products  4.36 us (2%)
  local copies, waits for them, and re-layouts  4.3 us (2%)
    pallas_call x1, Pallas kernels, main_call(): pl.pallas_call(functools.partial(main_kernel, block), in_specs=[pl.BlockS...  155 us
    pallas_call x1, Pallas kernels, sum_call(): pl.pallas_call(sum_kernel, in_specs=[vmem, vmem], out_specs=[hbm, hbm, vm...  65.3 us
    pallas_call x1, Pallas kernels, store_call(): pl.pallas_call(functools.partial(store_kernel, total_rows), in_specs=[sme...  5.17 us

profile of v8, /device:TPU:1, one launch (start us, length us, event | category | flops | bytes accessed | tf_op | source)
XLA Modules:
  0.0 238.7 jit_solution(4092333878206499235)
XLA Ops:
  0.6 0.0 copy-start.5
  0.6 0.0 copy-start.6
  2.1 0.6 pad_maximum_fusion.scal
  2.7 3.8 %multiply_reduce_fusion.1 = (f32[256]{0:T(256)S(1)}, f32[256,1024]{1,0:T(8,128)S(1)}) fusion(bf16[256,2048]{1,0:T(8,128)(2,1)} %img_x.1, bf16[2048,1024]{1,0:T(8,128)(2,1)} %param.8), kind=kOutput, calls=%fused_computation.3 | convolution fusion | flops 1074265856 | bytes 6292480 | tf_op jit(solution)/shard_map/dot_general | solution.py:18
  6.5 0.0 copy-start.4
  6.5 0.0 copy-done.5
  6.5 0.0 copy-done.6
  6.6 0.5 multiply_reduce_fusion
  7.1 0.0 copy-start.3
  7.1 1.0 copy-done.3
  8.1 1.2 multiply_convert_fusion
  9.2 0.0 copy-done.4
  9.2 155.5 %scores.1 = (f32[3,8,128]{2,1,0:T(8,128)}, bf16[256,6656]{1,0:T(8,128)(2,1)}) custom-call(f32[3]{0:T(128)} %pad_maximum_fusion.scal, bf16[256,1024]{1,0:T(8,128)(2,1)} %get-tuple-element.20.img_own, bf16[256,1024]{1,0:T(8,128)(2,1)} %get-tuple-element.19.txt_own, bf16[256,2048]{1,0:T(8,128)(2,1)} %img_x.1, bf16[256,512]{1,0:T(8,128)(2,1)} %txt_x.1, ...), custom_call_target="tpu_custom_call" | custom-call | tf_op jit(solution)/shard_map/scores/pallas_call | solution.py:526
  164.7 0.0 copy-start
  164.7 2.0 copy-done
  166.7 0.0 copy-start.1
  166.7 0.7 copy-done.1
  167.4 65.3 %weights.1 = (f32[2048,1024]{1,0:T(8,128)S(1)}, f32[512,1024]{1,0:T(8,128)S(1)}, f32[3,8,128]{2,1,0:T(8,128)S(1)}) custom-call(bf16[256,6656]{1,0:T(8,128)(2,1)S(1)} %copy-done, f32[3,8,128]{2,1,0:T(8,128)S(1)} %copy-done.1), custom_call_target="tpu_custom_call" | custom-call | tf_op jit(solution)/shard_map/weights/pallas_call | solution.py:728
  232.7 0.0 copy-start.2
  232.7 0.6 copy-done.2
  233.3 5.2 %store.1 = (f32[1]{0:T(128)}, f32[1]{0:T(128)}, f32[1]{0:T(128)}, f32[2048,1024]{1,0:T(8,128)}, f32[512,1024]{1,0:T(8,128)}) custom-call(f32[3]{0:T(128)S(1)} %copy-done.2, f32[3,8,128]{2,1,0:T(8,128)S(1)} %get-tuple-element.12.sums, f32[2048,1024]{1,0:T(8,128)S(1)} %get-tuple-element.13.src_a, f32[512,1024]{1,0:T(8,128)S(1)} %get-tuple-element.14.src_b), custom_call_target="tpu_custom_call" | custom-call | tf_op jit(solution)/shard_map/store/pallas_call | solution.py:766
  (2 shorter events, 0.0 us)
Async XLA Ops:
  0.6 5.9 %copy-start.5 = (bf16[256,512]{1,0:T(8,128)(2,1)S(1)}, bf16[256,512]{1,0:T(8,128)(2,1)}, u32[]{:S(2)}) copy-start(bf16[256,512]{1,0:T(8,128)(2,1)} %txt_x.1) | copy-start | bytes 786436
  0.6 5.9 %copy-start.6 = (bf16[512,1024]{1,0:T(8,128)(2,1)S(1)}, bf16[512,1024]{1,0:T(8,128)(2,1)}, u32[]{:S(2)}) copy-start(bf16[512,1024]{1,0:T(8,128)(2,1)} %param.9) | copy-start | bytes 3145732
  6.5 2.7 %copy-start.4 = (f32[256,1024]{1,0:T(8,128)}, f32[256,1024]{1,0:T(8,128)S(1)}, u32[]{:S(2)}) copy-start(f32[256,1024]{1,0:T(8,128)S(1)} %get-tuple-element.16.img_raw) | copy-start | bytes 3145732
  7.1 1.0 copy-start.3
  164.7 2.0 copy-start
  166.7 0.7 copy-start.1
  232.7 0.7 copy-start.2

commit v9 on v8

--- a/solution.py
+++ b/solution.py
@@ -459,7 +459,7 @@
         10: [lambda: take_chunk(2), rt.opposite],
         11: [ri.opposite],
         13: [lambda: give_chunk(1)],
-        14: [lambda: take_chunk(1), rt.early, ri.early],
+        14: [ri.early, lambda: take_chunk(1), rt.early],
     }
     score(0, 0)
     score(0, 1)

time: 239 us -> 239 us (level)
  no operation moved by 1% of the time
where the time goes in v9:
time: 239 us
  Pallas kernels  226 us (95%)
  matrix products  4.36 us (2%)
  local copies, waits for them, and re-layouts  4.3 us (2%)
    pallas_call x1, Pallas kernels, main_call(): pl.pallas_call(functools.partial(main_kernel, block), in_specs=[pl.BlockS...  155 us
    pallas_call x1, Pallas kernels, sum_call(): pl.pallas_call(sum_kernel, in_specs=[vmem, vmem], out_specs=[hbm, hbm, vm...  65.3 us
    pallas_call x1, Pallas kernels, store_call(): pl.pallas_call(functools.partial(store_kernel, total_rows), in_specs=[sme...  5.17 us

profile of v9, /device:TPU:1, one launch (start us, length us, event | category | flops | bytes accessed | tf_op | source)
XLA Modules:
  0.0 238.7 jit_solution(2526654683729046143)
XLA Ops:
  0.6 0.0 copy-start.5
  0.6 0.0 copy-start.6
  2.1 0.6 pad_maximum_fusion.scal
  2.7 3.8 %multiply_reduce_fusion.1 = (f32[256]{0:T(256)S(1)}, f32[256,1024]{1,0:T(8,128)S(1)}) fusion(bf16[256,2048]{1,0:T(8,128)(2,1)} %img_x.1, bf16[2048,1024]{1,0:T(8,128)(2,1)} %param.8), kind=kOutput, calls=%fused_computation.3 | convolution fusion | flops 1074265856 | bytes 6292480 | tf_op jit(solution)/shard_map/dot_general | solution.py:18
  6.5 0.0 copy-start.4
  6.5 0.0 copy-done.5
  6.5 0.0 copy-done.6
  6.6 0.5 multiply_reduce_fusion
  7.1 0.0 copy-start.3
  7.1 1.0 copy-done.3
  8.1 1.2 multiply_convert_fusion
  9.2 0.0 copy-done.4
  9.2 155.5 %scores.1 = (f32[3,8,128]{2,1,0:T(8,128)}, bf16[256,6656]{1,0:T(8,128)(2,1)}) custom-call(f32[3]{0:T(128)} %pad_maximum_fusion.scal, bf16[256,1024]{1,0:T(8,128)(2,1)} %get-tuple-element.20.img_own, bf16[256,1024]{1,0:T(8,128)(2,1)} %get-tuple-element.19.txt_own, bf16[256,2048]{1,0:T(8,128)(2,1)} %img_x.1, bf16[256,512]{1,0:T(8,128)(2,1)} %txt_x.1, ...), custom_call_target="tpu_custom_call" | custom-call | tf_op jit(solution)/shard_map/scores/pallas_call | solution.py:526
  164.7 0.0 copy-start
  164.7 2.0 copy-done
  166.7 0.0 copy-start.1
  166.7 0.7 copy-done.1
  167.4 65.3 %weights.1 = (f32[2048,1024]{1,0:T(8,128)S(1)}, f32[512,1024]{1,0:T(8,128)S(1)}, f32[3,8,128]{2,1,0:T(8,128)S(1)}) custom-call(bf16[256,6656]{1,0:T(8,128)(2,1)S(1)} %copy-done, f32[3,8,128]{2,1,0:T(8,128)S(1)} %copy-done.1), custom_call_target="tpu_custom_call" | custom-call | tf_op jit(solution)/shard_map/weights/pallas_call | solution.py:728
  232.7 0.0 copy-start.2
  232.7 0.6 copy-done.2
  233.3 5.2 %store.1 = (f32[1]{0:T(128)}, f32[1]{0:T(128)}, f32[1]{0:T(128)}, f32[2048,1024]{1,0:T(8,128)}, f32[512,1024]{1,0:T(8,128)}) custom-call(f32[3]{0:T(128)S(1)} %copy-done.2, f32[3,8,128]{2,1,0:T(8,128)S(1)} %get-tuple-element.12.sums, f32[2048,1024]{1,0:T(8,128)S(1)} %get-tuple-element.13.src_a, f32[512,1024]{1,0:T(8,128)S(1)} %get-tuple-element.14.src_b), custom_call_target="tpu_custom_call" | custom-call | tf_op jit(solution)/shard_map/store/pallas_call | solution.py:766
  (2 shorter events, 0.0 us)
Async XLA Ops:
  0.6 5.9 %copy-start.5 = (bf16[256,512]{1,0:T(8,128)(2,1)S(1)}, bf16[256,512]{1,0:T(8,128)(2,1)}, u32[]{:S(2)}) copy-start(bf16[256,512]{1,0:T(8,128)(2,1)} %txt_x.1) | copy-start | bytes 786436
  0.6 5.9 %copy-start.6 = (bf16[512,1024]{1,0:T(8,128)(2,1)S(1)}, bf16[512,1024]{1,0:T(8,128)(2,1)}, u32[]{:S(2)}) copy-start(bf16[512,1024]{1,0:T(8,128)(2,1)} %param.9) | copy-start | bytes 3145732
  6.5 2.7 %copy-start.4 = (f32[256,1024]{1,0:T(8,128)}, f32[256,1024]{1,0:T(8,128)S(1)}, u32[]{:S(2)}) copy-start(f32[256,1024]{1,0:T(8,128)S(1)} %get-tuple-element.16.img_raw) | copy-start | bytes 3145732
  7.1 1.0 copy-start.3
  164.7 2.0 copy-start
  166.7 0.7 copy-start.1
  232.7 0.7 copy-start.2
